TPU v7x, 1024 devices: a whole 4x4x32 slice. The times are simulated.
1024 devices in a mesh: pipe: 32 (over x, z_lo), expert: 32 (over y, z_hi, core).
Axes of the slice: x: 4, y: 4, z: 32 (z_hi: 4, z_lo: 8; z = z_hi * 8 + z_lo), core: 2. Of those that a mesh axis runs over, the one named last changes fastest.
Arguments:
- forward_in: bfloat16 [32, 2048, 3584], P('pipe', 'expert'), may hold values from -6 to 6
- forward_ids: int32 [32, 2048, 1], P('pipe', 'expert'), may hold values from 0 to 7, as said below
- forward_gates: float32 [32, 2048, 1], P('pipe', 'expert'), may hold values from 0.4 to 1
- grad_in: bfloat16 [32, 2048, 3584], P('pipe', 'expert'), may hold values from -6 to 6
- grad_ids: int32 [32, 2048, 1], P('pipe', 'expert'), may hold values from 0 to 7, as said below
- grad_gates: float32 [32, 2048, 1], P('pipe', 'expert'), may hold values from 0.4 to 1
- saved_input: bfloat16 [32, 2048, 3584], P('pipe', 'expert'), may hold values from -6 to 6
- saved_acts: bfloat16 [32, 32, 256, 512], P('pipe', 'expert'), may hold values from -8 to 8
- norm_gain: float32 [32, 3584], P('pipe'), may hold values from 0.1 to 1.9
- weight_in: bfloat16 [32, 3584, 512], P('expert'), may hold values from -0.09375 to 0.09375
- weight_out: bfloat16 [32, 256, 3584], P('expert'), may hold values from -0.1875 to 0.1875
Outputs:
- forward_out: bfloat16 [32, 2048, 3584], P('pipe', 'expert')
- grad_out: bfloat16 [32, 2048, 3584], P('pipe', 'expert')
Inputs may be any that keep to these rules, and one draw needn't show every extreme that they name: `forward_ids`: A token's 1 ids are distinct; for each section, the 64 tokens of one device name every expert exactly 8 times. `grad_ids`: A token's 1 ids are distinct; for each section, the 64 tokens of one device name every expert exactly 8 times.
All inputs are finite; a program needn't handle non-finite values.
Results may differ from a plain program's by a relative error of at most 0.008.
Values may be sent and summed in bfloat16 or wider, within the bound.
No kernel may reach another device: no remote copies, remote signals or barrier semaphores. Data moves between devices by JAX's collectives and lax.ppermute only.
A program may use at most 32 MiB of HBM per device.

v0:
```python
import jax
import jax.numpy as jnp
from jax import lax
from jax.sharding import PartitionSpec as P

epsilon = 1e-06


def passed_along(array, axis, by):
    peers = lax.axis_size(axis)
    return lax.ppermute(array, axis, [(i, (i + by) % peers) for i in range(peers)])


def normalize(tokens, norm_scale):
    widened = tokens.astype(jnp.float32)
    inverse_rms = lax.rsqrt(jnp.mean(widened * widened, axis=-1, keepdims=True) + epsilon)
    return (widened * inverse_rms * norm_scale).astype(jnp.bfloat16)


def slot_order(route_ids):
    flattened = route_ids.reshape(-1)
    sorted_pairs = jnp.argsort(flattened, stable=True)
    inverse_pairs = jnp.argsort(sorted_pairs, stable=True)
    return (sorted_pairs, inverse_pairs)


def deliver(grouped, group_size):
    outgoing = jnp.repeat(grouped, group_size, axis=0)
    return lax.all_to_all(outgoing, "expert", split_axis=0, concat_axis=0, tiled=True)


def collect(partial_rows, expert_count, group_size):
    slices_total, capacity, model_width = partial_rows.shape
    arrived = lax.all_to_all(partial_rows, "expert", split_axis=0, concat_axis=0, tiled=True)
    summed = jnp.sum(
        arrived.reshape(expert_count, group_size, capacity, model_width).astype(jnp.float32), axis=1
    )
    return summed.reshape(expert_count * capacity, model_width)


def on_device(
    forward_in,
    forward_ids,
    forward_gates,
    grad_in,
    grad_ids,
    grad_gates,
    saved_input,
    saved_acts,
    norm_gain,
    weight_in,
    weight_out,
):
    tokens = forward_in[0]
    sources = lax.axis_size("expert")
    token_count, top_count = forward_ids[0].shape
    model_width = tokens.shape[1]
    group_size = min(4, sources // 2)
    expert_count = sources // group_size
    capacity = token_count * top_count // expert_count
    norm_scale = norm_gain[0]
    w_first = weight_in[0]
    w_second = weight_out[0]
    hidden_width = w_second.shape[0]
    normed = normalize(tokens, norm_scale)
    fwd_sorted, fwd_inverse = slot_order(forward_ids[0])
    grad_sorted, grad_inverse = slot_order(grad_ids[0])
    fwd_grouped = jnp.take(normed, fwd_sorted // top_count, axis=0).reshape(
        expert_count, capacity, model_width
    )
    grad_grouped = jnp.take(grad_in[0], grad_sorted // top_count, axis=0).reshape(
        expert_count, capacity, model_width
    )
    fwd_arrived = deliver(fwd_grouped, group_size)
    projected = jnp.einsum("scd,df->scf", fwd_arrived, w_first, preferred_element_type=jnp.float32)
    hidden = (jax.nn.silu(projected[..., :hidden_width]) * projected[..., hidden_width:]).astype(
        jnp.bfloat16
    )
    fwd_partial = jnp.einsum(
        "scf,fd->scd", hidden, w_second, preferred_element_type=jnp.float32
    ).astype(jnp.bfloat16)
    fwd_flat = collect(fwd_partial, expert_count, group_size)
    grad_arrived = deliver(grad_grouped, group_size)
    stored = saved_acts[0].reshape(sources, capacity, 2 * hidden_width)
    hidden_grad = jnp.einsum(
        "scd,fd->scf", grad_arrived, w_second, preferred_element_type=jnp.float32
    )
    gate_act = stored[..., :hidden_width].astype(jnp.float32)
    up_act = stored[..., hidden_width:].astype(jnp.float32)
    squashed = jax.nn.sigmoid(gate_act)
    gate_grad = (hidden_grad * up_act * squashed * (1.0 + gate_act * (1.0 - squashed))).astype(
        jnp.bfloat16
    )
    up_grad = (hidden_grad * gate_act * squashed).astype(jnp.bfloat16)
    joined = jnp.concatenate([gate_grad, up_grad], axis=-1)
    grad_partial = jnp.einsum(
        "scf,df->scd", joined, w_first, preferred_element_type=jnp.float32
    ).astype(jnp.bfloat16)
    grad_flat = collect(grad_partial, expert_count, group_size)
    fwd_pairs = jnp.take(fwd_flat, fwd_inverse, axis=0).reshape(token_count, top_count, model_width)
    combined = jnp.einsum("tk,tkd->td", forward_gates[0], fwd_pairs)
    moved = (tokens.astype(jnp.float32) + combined).astype(jnp.bfloat16)
    grad_pairs = jnp.take(grad_flat, grad_inverse, axis=0).reshape(
        token_count, top_count, model_width
    )
    pulled = jnp.einsum("tk,tkd->td", grad_gates[0], grad_pairs)
    widened = saved_input[0].astype(jnp.float32)
    inverse_rms = lax.rsqrt(jnp.mean(widened * widened, axis=-1, keepdims=True) + epsilon)
    unit_rows = widened * inverse_rms
    weighted = pulled * norm_scale
    through = grad_in[0].astype(jnp.float32) + inverse_rms * (
        weighted - unit_rows * jnp.mean(weighted * unit_rows, axis=-1, keepdims=True)
    )
    through = through.astype(jnp.bfloat16)
    forward_out = passed_along(moved[None], "pipe", 1)
    grad_out = passed_along(through[None], "pipe", -1)
    return (forward_out, grad_out)


def solution(mesh):
    placed = (
        P("pipe", "expert", None),
        P("pipe", "expert", None),
        P("pipe", "expert", None),
        P("pipe", "expert", None),
        P("pipe", "expert", None),
        P("pipe", "expert", None),
        P("pipe", "expert", None),
        P("pipe", "expert", None, None),
        P("pipe", None),
        P("expert", None, None),
        P("expert", None, None),
    )
    return jax.shard_map(
        on_device,
        mesh=mesh,
        in_specs=placed,
        out_specs=(P("pipe", "expert", None), P("pipe", "expert", None)),
        check_vma=False,
    )
```

profile of v0, /device:TPU:1, one launch (start us, length us, event | category | flops | bytes accessed | tf_op | source)
XLA Modules:
  0.0 789.4 jit_solution(17285840331165371196)
XLA Ops:
  0.7 2.8 sort.61
  3.5 2.4 gather_fusion.2
  6.1 199.3 %all_to_all.20 = bf16[32,8,3584]{2,1,0:T(8,128)(2,1)S(1)} all-to-all(bf16[32,8,3584]{2,1,0:T(8,128)(2,1)S(1)} %bitcast.54), channel_id=1, replica_groups=mesh['pipe'=32,'expert'=32] {'expert'}, dimensions={0} | all-to-all | bytes 3670016 | tf_op jit(solution)/shard_map/all_to_all | solution.py:29
  205.4 0.7 fusion.26
  206.1 1.3 copy-done.6
  207.5 2.4 convolution_convert_fusion
  209.9 16.1 %all-to-all-start.3 = ((bf16[32,8,3584]{2,1,0:T(8,128)(2,1)}), bf16[32,8,3584]{2,1,0:T(8,128)(2,1)}, u32[]{:S(2)}, u32[]{:S(2)}) async-start(bf16[32,8,3584]{2,1,0:T(8,128)(2,1)} %convolution_convert_fusion), calls=%async_computation.3 | async-start | bytes 3670016 | tf_op jit(solution)/shard_map/all_to_all | solution.py:34
  226.0 2.0 sort.62
  228.1 2.0 sort.59
  230.2 0.2 fusion.13
  230.4 0.2 fusion.14
  230.6 158.6 %all-to-all-done.3 = bf16[32,8,3584]{2,1,0:T(8,128)(2,1)} async-done(((bf16[32,8,3584]{2,1,0:T(8,128)(2,1)}), bf16[32,8,3584]{2,1,0:T(8,128)(2,1)}, u32[]{:S(2)}, u32[]{:S(2)}) %all-to-all-start.3) | async-done | bytes 1835040 | tf_op jit(solution)/shard_map/all_to_all | solution.py:34
  389.2 1.9 convert_reduce_fusion
  391.1 1.8 gather_fusion.3
  392.9 1.8 fusion.8
  394.7 2.4 fusion.20
  397.1 0.8 gather_fusion
  398.2 179.3 %all_to_all.21 = bf16[32,8,3584]{2,1,0:T(8,128)(2,1)S(1)} all-to-all(bf16[32,8,3584]{2,1,0:T(8,128)(2,1)S(1)} %bitcast.55), channel_id=1, replica_groups=mesh['pipe'=32,'expert'=32] {'expert'}, dimensions={0} | all-to-all | bytes 3670016 | tf_op jit(solution)/shard_map/all_to_all | solution.py:29
  577.5 1.1 fusion.1
  578.6 1.9 convolution_convert_fusion.1
  580.5 13.8 %all-to-all-start.1 = ((bf16[32,8,3584]{2,1,0:T(8,128)(2,1)}), bf16[32,8,3584]{2,1,0:T(8,128)(2,1)}, u32[]{:S(2)}, u32[]{:S(2)}) async-start(bf16[32,8,3584]{2,1,0:T(8,128)(2,1)} %convolution_convert_fusion.1), calls=%async_computation.1 | async-start | bytes 3670016 | tf_op jit(solution)/shard_map/all_to_all | solution.py:34
  594.4 2.0 sort.60
  596.4 2.3 collective-permute-start.1
  598.7 109.0 %all-to-all-done.1 = bf16[32,8,3584]{2,1,0:T(8,128)(2,1)} async-done(((bf16[32,8,3584]{2,1,0:T(8,128)(2,1)}), bf16[32,8,3584]{2,1,0:T(8,128)(2,1)}, u32[]{:S(2)}, u32[]{:S(2)}) %all-to-all-start.1) | async-done | bytes 1835040 | tf_op jit(solution)/shard_map/all_to_all | solution.py:34
  707.7 1.9 convert_reduce_fusion.1
  709.6 1.8 gather_fusion.1
  711.4 1.4 fusion.19
  712.8 14.7 %collective-permute-start = (bf16[1,64,3584]{2,1,0:T(8,128)(2,1)S(1)}, bf16[1,64,3584]{2,1,0:T(8,128)(2,1)S(1)}, u32[]{:S(2)}, u32[]{:S(2)}) collective-permute-start(bf16[1,64,3584]{2,1,0:T(8,128)(2,1)S(1)} %fusion.19), channel_id=1, source_target_pairs={{0,32},{32,64},{64,96},{96,128},{128,160},{160,192},{192,224},{224... | collective-permute-start | bytes 1376264 | tf_op jit(solution)/shard_map/ppermute | solution.py:11
  727.4 35.1 %collective-permute-done.1 = bf16[1,64,3584]{2,1,0:T(8,128)(2,1)} collective-permute-done((bf16[1,64,3584]{2,1,0:T(8,128)(2,1)}, bf16[1,64,3584]{2,1,0:T(8,128)(2,1)}, u32[]{:S(2)}, u32[]{:S(2)}) %collective-permute-start.1) | collective-permute-done | bytes 458784 | tf_op jit(solution)/shard_map/ppermute | solution.py:11
  762.6 24.3 %collective-permute-done = bf16[1,64,3584]{2,1,0:T(8,128)(2,1)S(1)} collective-permute-done((bf16[1,64,3584]{2,1,0:T(8,128)(2,1)S(1)}, bf16[1,64,3584]{2,1,0:T(8,128)(2,1)S(1)}, u32[]{:S(2)}, u32[]{:S(2)}) %collective-permute-start) | collective-permute-done | bytes 458784 | tf_op jit(solution)/shard_map/ppermute | solution.py:11
  786.9 0.8 copy.15
  787.6 1.8 copy.16
  (48 shorter events, 0.7 us)
Async XLA Ops:
  0.6 204.8 %copy-start = (bf16[1,256,3584]{2,1,0:T(8,128)(2,1)S(1)}, bf16[1,256,3584]{2,1,0:T(8,128)(2,1)}, u32[]{:S(2)}) copy-start(bf16[1,256,3584]{2,1,0:T(8,128)(2,1)} %param.25) | copy-start | bytes 5505028
  6.1 199.3 %copy-start.11 = (bf16[1,1,256,512]{3,2,1,0:T(8,128)(2,1)S(1)}, bf16[1,1,256,512]{3,2,1,0:T(8,128)(2,1)}, u32[]{:S(2)}) copy-start(bf16[1,1,256,512]{3,2,1,0:T(8,128)(2,1)} %param.22) | copy-start | bytes 786436
  205.4 2.0 copy-start.6
  209.9 18.2 %copy-start.8 = (f32[1,3584]{1,0:T(1,128)S(1)}, f32[1,3584]{1,0:T(1,128)}, u32[]{:S(2)}) copy-start(f32[1,3584]{1,0:T(1,128)} %param.23) | copy-start | bytes 43012
  209.9 18.2 %copy-start.12 = (s32[1,64,1]{1,2,0:T(1,128)S(1)}, s32[1,64,1]{1,2,0:T(1,128)}, u32[]{:S(2)}) copy-start(s32[1,64,1]{1,2,0:T(1,128)} %param.16) | copy-start | bytes 772
  209.9 20.3 %copy-start.5 = (bf16[1,64,3584]{2,1,0:T(8,128)(2,1)S(1)}, bf16[1,64,3584]{2,1,0:T(8,128)(2,1)}, u32[]{:S(2)}) copy-start(bf16[1,64,3584]{2,1,0:T(8,128)(2,1)} %param.21) | copy-start | bytes 1376260
  209.9 20.5 %copy-start.3 = (bf16[1,64,3584]{2,1,0:T(8,128)(2,1)S(1)}, bf16[1,64,3584]{2,1,0:T(8,128)(2,1)}, u32[]{:S(2)}) copy-start(bf16[1,64,3584]{2,1,0:T(8,128)(2,1)} %param.15) | copy-start | bytes 1376260
  209.9 179.4 %all-to-all-start.3 = ((bf16[32,8,3584]{2,1,0:T(8,128)(2,1)}), bf16[32,8,3584]{2,1,0:T(8,128)(2,1)}, u32[]{:S(2)}, u32[]{:S(2)}) async-start(bf16[32,8,3584]{2,1,0:T(8,128)(2,1)} %convolution_convert_fusion), calls=%async_computation.3 | async-start | bytes 3670016 | tf_op jit(solution)/shard_map/all_to_all | solution.py:34
  391.1 1.8 copy-start.9
  391.1 3.6 copy-start.1
  392.9 1.8 copy-start.2
  398.2 179.3 %copy-start.7 = (bf16[1,3584,512]{2,1,0:T(8,128)(2,1)S(1)}, bf16[1,3584,512]{2,1,0:T(8,128)(2,1)}, u32[]{:S(2)}) copy-start(bf16[1,3584,512]{2,1,0:T(8,128)(2,1)} %param.24) | copy-start | bytes 11010052
  580.5 127.2 %all-to-all-start.1 = ((bf16[32,8,3584]{2,1,0:T(8,128)(2,1)}), bf16[32,8,3584]{2,1,0:T(8,128)(2,1)}, u32[]{:S(2)}, u32[]{:S(2)}) async-start(bf16[32,8,3584]{2,1,0:T(8,128)(2,1)} %convolution_convert_fusion.1), calls=%async_computation.1 | async-start | bytes 3670016 | tf_op jit(solution)/shard_map/all_to_all | solution.py:34
  596.4 166.2 %collective-permute-start.1 = (bf16[1,64,3584]{2,1,0:T(8,128)(2,1)}, bf16[1,64,3584]{2,1,0:T(8,128)(2,1)}, u32[]{:S(2)}, u32[]{:S(2)}) collective-permute-start(bf16[1,64,3584]{2,1,0:T(8,128)(2,1)} %get-tuple-element.14), channel_id=1, source_target_pairs={{0,992},{32,0},{64,32},{96,64},{128,96},{160,128},{192,160},{224,1... | collective-permute-start | bytes 1376264 | tf_op jit(solution)/shard_map/ppermute | solution.py:11
  709.6 1.8 copy-start.4
  709.6 1.8 copy-start.10
  712.8 74.1 %collective-permute-start = (bf16[1,64,3584]{2,1,0:T(8,128)(2,1)S(1)}, bf16[1,64,3584]{2,1,0:T(8,128)(2,1)S(1)}, u32[]{:S(2)}, u32[]{:S(2)}) collective-permute-start(bf16[1,64,3584]{2,1,0:T(8,128)(2,1)S(1)} %fusion.19), channel_id=1, source_target_pairs={{0,32},{32,64},{64,96},{96,128},{128,160},{160,192},{192,224},{224... | collective-permute-start | bytes 1376264 | tf_op jit(solution)/shard_map/ppermute | solution.py:11
where the time goes:
time: 801 us; the launch traced here: 789 us
  blocking collectives  379 us (47%)
  waiting for transfers between devices  327 us (41%)
  starting transfers between devices  46.9 us (6%)
  other arithmetic  18.9 us (2%)
  local copies, waits for them, and re-layouts  11 us (1%)
    all_to_all x2, blocking collectives, deliver(): lax.all_to_all(outgoing, 'expert', split_axis=0, concat_axis=0, tiled=True)  379 us
    all_to_all x2, waiting for transfers between devices, collect(): lax.all_to_all(partial_rows, 'expert', split_axis=0, concat_axis=0, tiled...  268 us
    ppermute x2, waiting for transfers between devices, passed_along(): lax.ppermute(array, axis, [(i, (i + by) % peers) for i in range(peers)])  59.4 us
    all_to_all x2, starting transfers between devices, collect(): lax.all_to_all(partial_rows, 'expert', split_axis=0, concat_axis=0, tiled...  30 us
    ppermute x2, starting transfers between devices, passed_along(): lax.ppermute(array, axis, [(i, (i + by) % peers) for i in range(peers)])  16.9 us
  transfers between devices with their start and end apart: 4, of which 4 were waited for; matrix products, arithmetic and copies ran while one was open for 1% of the time, Pallas kernels for 0%

commit v1 on v0

v1 whole, which is shorter than its diff:
```python
import jax
import jax.numpy as jnp
from jax import lax
from jax.sharding import Mesh, PartitionSpec as P

epsilon = 1e-06
PLANE = ("x", "y", "c")
RING = ("zh", "zl")


def normalize(tokens, norm_scale):
    widened = tokens.astype(jnp.float32)
    inverse_rms = lax.rsqrt(jnp.mean(widened * widened, axis=-1, keepdims=True) + epsilon)
    return (widened * inverse_rms * norm_scale).astype(jnp.bfloat16)


def slot_order(route_ids):
    flattened = route_ids.reshape(-1)
    sorted_pairs = jnp.argsort(flattened, stable=True)
    inverse_pairs = jnp.argsort(sorted_pairs, stable=True)
    return (sorted_pairs, inverse_pairs)


def swapped(parts):
    parts = lax.all_to_all(parts, "zh", split_axis=0, concat_axis=0, tiled=True)
    return lax.all_to_all(parts, "x", split_axis=0, concat_axis=0, tiled=True)


def moved_weight(weight):
    rows, columns = weight.shape
    blocks, run, across = lax.axis_size("zh"), lax.axis_size("zl"), lax.axis_size("x")
    height, width = rows // (blocks * run), columns // across
    cut = weight.reshape(blocks, run, height, columns)
    mine = lax.dynamic_slice(
        cut,
        (0, lax.axis_index("zl"), 0, lax.axis_index("x") * width),
        (blocks, 1, height, width),
    )[:, 0]
    strips = swapped(mine)
    part = strips.transpose(1, 0, 2).reshape(height, columns)
    return lax.all_gather(part, RING, axis=0, tiled=True)


def deliver(grouped):
    experts, capacity, width = grouped.shape
    ys, cs = lax.axis_size("y"), lax.axis_size("c")
    pairs = experts // ys
    half = lax.axis_size("x") // pairs
    by_place = grouped.reshape(ys, pairs, capacity, width).transpose(1, 0, 2, 3)
    outgoing = jnp.broadcast_to(
        by_place[:, None, :, None], (pairs, half, ys, cs, capacity, width)
    ).reshape(pairs * half * ys * cs, capacity, width)
    return lax.all_to_all(outgoing, PLANE, split_axis=0, concat_axis=0, tiled=True)


def collect(partial_rows, experts):
    slices, capacity, width = partial_rows.shape
    ys, cs = lax.axis_size("y"), lax.axis_size("c")
    pairs = experts // ys
    half = lax.axis_size("x") // pairs
    arrived = lax.all_to_all(partial_rows, PLANE, split_axis=0, concat_axis=0, tiled=True)
    summed = jnp.sum(
        arrived.reshape(pairs, half, ys, cs, capacity, width).astype(jnp.float32), axis=(1, 3)
    )
    return summed.transpose(1, 0, 2, 3).reshape(experts * capacity, width)


def shifted(array, by):
    sections = lax.axis_size(("x", "zl"))
    return lax.ppermute(array, ("x", "zl"), [(i, (i + by) % sections) for i in range(sections)])


def on_device(
    forward_in,
    forward_ids,
    forward_gates,
    grad_in,
    grad_ids,
    grad_gates,
    saved_input,
    saved_acts,
    norm_gain,
    weight_in,
    weight_out,
):
    tokens = forward_in[0]
    sources = lax.axis_size(("y", "zh", "c"))
    token_count, top_count = forward_ids[0].shape
    model_width = tokens.shape[1]
    group_size = min(4, sources // 2)
    expert_count = sources // group_size
    capacity = token_count * top_count // expert_count
    norm_scale = norm_gain[0]
    hidden_width = weight_out.shape[1]

    w_first = moved_weight(weight_in[0])
    w_second = moved_weight(weight_out[0])
    ys, blocks, cs = lax.axis_size("y"), lax.axis_size("zh"), lax.axis_size("c")
    acts = saved_acts[0, 0].reshape(ys, blocks, cs * capacity, 2 * hidden_width)
    acts = acts.transpose(1, 0, 2, 3).reshape(blocks, ys * cs * capacity, 2 * hidden_width)
    stored = swapped(acts).reshape(-1, capacity, 2 * hidden_width)

    normed = normalize(tokens, norm_scale)
    fwd_sorted, fwd_inverse = slot_order(forward_ids[0])
    grad_sorted, grad_inverse = slot_order(grad_ids[0])
    fwd_grouped = jnp.take(normed, fwd_sorted // top_count, axis=0).reshape(
        expert_count, capacity, model_width
    )
    grad_grouped = jnp.take(grad_in[0], grad_sorted // top_count, axis=0).reshape(
        expert_count, capacity, model_width
    )
    fwd_arrived = deliver(fwd_grouped)
    grad_arrived = deliver(grad_grouped)

    projected = jnp.einsum("scd,df->scf", fwd_arrived, w_first, preferred_element_type=jnp.float32)
    hidden = (jax.nn.silu(projected[..., :hidden_width]) * projected[..., hidden_width:]).astype(
        jnp.bfloat16
    )
    fwd_partial = jnp.einsum(
        "scf,fd->scd", hidden, w_second, preferred_element_type=jnp.float32
    ).astype(jnp.bfloat16)
    fwd_flat = collect(fwd_partial, expert_count)

    hidden_grad = jnp.einsum(
        "scd,fd->scf", grad_arrived, w_second, preferred_element_type=jnp.float32
    )
    gate_act = stored[..., :hidden_width].astype(jnp.float32)
    up_act = stored[..., hidden_width:].astype(jnp.float32)
    squashed = jax.nn.sigmoid(gate_act)
    gate_grad = (hidden_grad * up_act * squashed * (1.0 + gate_act * (1.0 - squashed))).astype(
        jnp.bfloat16
    )
    up_grad = (hidden_grad * gate_act * squashed).astype(jnp.bfloat16)
    joined = jnp.concatenate([gate_grad, up_grad], axis=-1)
    grad_partial = jnp.einsum(
        "scf,df->scd", joined, w_first, preferred_element_type=jnp.float32
    ).astype(jnp.bfloat16)
    grad_flat = collect(grad_partial, expert_count)

    fwd_pairs = jnp.take(fwd_flat, fwd_inverse, axis=0).reshape(token_count, top_count, model_width)
    combined = jnp.einsum("tk,tkd->td", forward_gates[0], fwd_pairs)
    moved = (tokens.astype(jnp.float32) + combined).astype(jnp.bfloat16)
    grad_pairs = jnp.take(grad_flat, grad_inverse, axis=0).reshape(
        token_count, top_count, model_width
    )
    pulled = jnp.einsum("tk,tkd->td", grad_gates[0], grad_pairs)
    widened = saved_input[0].astype(jnp.float32)
    inverse_rms = lax.rsqrt(jnp.mean(widened * widened, axis=-1, keepdims=True) + epsilon)
    unit_rows = widened * inverse_rms
    weighted = pulled * norm_scale
    through = grad_in[0].astype(jnp.float32) + inverse_rms * (
        weighted - unit_rows * jnp.mean(weighted * unit_rows, axis=-1, keepdims=True)
    )
    through = through.astype(jnp.bfloat16)
    return (shifted(moved[None], 1), shifted(through[None], -1))


def solution(mesh):
    fine = Mesh(mesh.devices.reshape(4, -1, 4, 4, 2), ("x", "zl", "y", "zh", "c"))
    pipe, expert = ("x", "zl"), ("y", "zh", "c")
    rows = P(pipe, expert, None)
    placed = (rows,) * 7 + (
        P(pipe, expert, None, None),
        P(pipe, None),
        P(expert, None, None),
        P(expert, None, None),
    )
    return jax.shard_map(
        on_device, mesh=fine, in_specs=placed, out_specs=(rows, rows), check_vma=False
    )
```

time: 801 us -> 493 us (0.62); the launches traced: 789 us -> 492 us
  blocking collectives: 379 us -> 163 us
  waiting for transfers between devices: 327 us -> 220 us
  between operations: 0.93 us -> 14.4 us
    all_to_all x2 -> x6, blocking collectives: 379 us -> 163 us  [the longest x2 76.1 us: swapped(): parts = lax.all_to_all(parts, 'zh', split_axis=0, concat_axis=0, tiled=True)]
    all_to_all x2 -> x4, waiting for transfers between devices: 268 us -> 67.2 us  [the longest x2 37.8 us: collect(): lax.all_to_all(partial_rows, PLANE, split_axis=0, concat_axis=0, tiled=True)]
    all_gather x0 -> x2, waiting for transfers between devices: none -> 130 us  [moved_weight(): return lax.all_gather(part, RING, axis=0, tiled=True)]
    ppermute x2, waiting for transfers between devices: 59.4 us -> 22.8 us  [shifted(): lax.ppermute(array, ('x', 'zl'), [(i, (i + by) % sections) for i in range...]
    all_to_all x2 -> x4, starting transfers between devices: 30 us -> 41.9 us  [the longest x2 33 us: collect(): lax.all_to_all(partial_rows, PLANE, split_axis=0, concat_axis=0, tiled=True)]
  transfers between devices with their start and end apart: 4 -> 8, of which waited for: 4 -> 7; matrix products, arithmetic and copies ran while one was open for 1% -> 4% of each run, Pallas kernels for 0% -> 0%
where the time goes in v1:
time: 493 us; the launch traced here: 492 us
  waiting for transfers between devices  220 us (45%)
  blocking collectives  163 us (33%)
  starting transfers between devices  52.8 us (11%)
  other arithmetic  18.3 us (4%)
  between operations  14.4 us (3%)
  local copies, waits for them, and re-layouts  13.4 us (3%)
  matrix products  10.3 us (2%)
    all_gather x2, waiting for transfers between devices, moved_weight(): return lax.all_gather(part, RING, axis=0, tiled=True)  130 us
    all_to_all x2, blocking collectives, swapped(): parts = lax.all_to_all(parts, 'zh', split_axis=0, concat_axis=0, tiled=True)  76.1 us
    all_to_all x2, blocking collectives, deliver(): lax.all_to_all(outgoing, PLANE, split_axis=0, concat_axis=0, tiled=True)  71 us
    all_to_all x2, waiting for transfers between devices, collect(): lax.all_to_all(partial_rows, PLANE, split_axis=0, concat_axis=0, tiled=True)  37.8 us
    all_to_all x2, starting transfers between devices, collect(): lax.all_to_all(partial_rows, PLANE, split_axis=0, concat_axis=0, tiled=True)  33 us
    all_to_all x1, waiting for transfers between devices, swapped(): parts = lax.all_to_all(parts, 'zh', split_axis=0, concat_axis=0, tiled=True)  23.7 us
    ppermute x2, waiting for transfers between devices, shifted(): lax.ppermute(array, ('x', 'zl'), [(i, (i + by) % sections) for i in range...  22.8 us
    all_to_all x2, blocking collectives, swapped(): return lax.all_to_all(parts, 'x', split_axis=0, concat_axis=0, tiled=True)  15.5 us
  transfers between devices with their start and end apart: 8, of which 7 were waited for; matrix products, arithmetic and copies ran while one was open for 4% of the time, Pallas kernels for 0%

profile of v1, /device:TPU:1, one launch (start us, length us, event | category | flops | bytes accessed | tf_op | source)
XLA Modules:
  0.0 491.8 jit_solution(11456352519463498992)
XLA Ops:
  8.7 50.7 %all_to_all.50 = bf16[4,8,896]{2,1,0:T(8,128)(2,1)S(1)} all-to-all(bf16[4,8,896]{2,1,0:T(8,128)(2,1)S(1)} %dynamic-slice_bitcast_fusion.1), channel_id=1, replica_groups=mesh['x'=4,'zl'=8,'y'=4,'zh'=4,'c'=2] {'zh'}, dimensions={0} | all-to-all | bytes 114688 | tf_op jit(solution)/shard_map/all_to_all | solution.py:25
  59.4 8.3 %all_to_all.51 = bf16[4,8,896]{2,1,0:T(8,128)(2,1)} all-to-all(bf16[4,8,896]{2,1,0:T(8,128)(2,1)S(1)} %all_to_all.50), channel_id=1, replica_groups=mesh['x'=4,'zl'=8,'y'=4,'zh'=4,'c'=2] {'x'}, dimensions={0} | all-to-all | bytes 114688 | tf_op jit(solution)/shard_map/all_to_all | solution.py:26
  68.8 25.4 %all_to_all.52 = bf16[4,112,128]{2,1,0:T(8,128)(2,1)S(1)} all-to-all(bf16[4,112,128]{2,1,0:T(8,128)(2,1)S(1)} %dynamic-slice_bitcast_fusion), channel_id=1, replica_groups=mesh['x'=4,'zl'=8,'y'=4,'zh'=4,'c'=2] {'zh'}, dimensions={0} | all-to-all | bytes 229376 | tf_op jit(solution)/shard_map/all_to_all | solution.py:25
  94.2 7.2 %all_to_all.53 = bf16[4,112,128]{2,1,0:T(8,128)(2,1)S(1)} all-to-all(bf16[4,112,128]{2,1,0:T(8,128)(2,1)S(1)} %all_to_all.52), channel_id=1, replica_groups=mesh['x'=4,'zl'=8,'y'=4,'zh'=4,'c'=2] {'x'}, dimensions={0} | all-to-all | bytes 229376 | tf_op jit(solution)/shard_map/all_to_all | solution.py:26
  103.7 4.1 all-to-all-start.7
  107.7 2.1 sort.61
  109.9 2.1 sort.62
  112.8 23.7 %all-to-all-done.7 = bf16[4,64,512]{2,1,0:T(8,128)(2,1)} async-done(((bf16[4,64,512]{2,1,0:T(8,128)(2,1)}), bf16[4,64,512]{2,1,0:T(8,128)(2,1)}, u32[]{:S(2)}, u32[]{:S(2)}) %all-to-all-start.7) | async-done | bytes 262176 | tf_op jit(solution)/shard_map/all_to_all | solution.py:25
  136.5 4.9 %all-to-all-start.8 = ((bf16[4,64,512]{2,1,0:T(8,128)(2,1)}), bf16[4,64,512]{2,1,0:T(8,128)(2,1)S(1)}, u32[]{:S(2)}, u32[]{:S(2)}) async-start(bf16[4,64,512]{2,1,0:T(8,128)(2,1)} %all-to-all-done.7), calls=%async_computation.8 | async-start | bytes 524288 | tf_op jit(solution)/shard_map/all_to_all | solution.py:26
  141.6 5.8 %all-to-all-done.8 = bf16[4,64,512]{2,1,0:T(8,128)(2,1)S(1)} async-done(((bf16[4,64,512]{2,1,0:T(8,128)(2,1)}), bf16[4,64,512]{2,1,0:T(8,128)(2,1)S(1)}, u32[]{:S(2)}, u32[]{:S(2)}) %all-to-all-start.8) | async-done | bytes 262176 | tf_op jit(solution)/shard_map/all_to_all | solution.py:26
  147.5 41.7 %all_to_all.54 = bf16[32,8,3584]{2,1,0:T(8,128)(2,1)} all-to-all(bf16[32,8,3584]{2,1,0:T(8,128)(2,1)S(1)} %bitcast.76), channel_id=1, replica_groups=mesh['x'=4,'zl'=8,'y'=4,'zh'=4,'c'=2] {'x','y','c'}, dimensions={0} | all-to-all | bytes 3670016 | tf_op jit(solution)/shard_map/all_to_all | solution.py:53
  189.8 2.7 fusion.26
  192.5 129.3 %all-gather.3.cloned.1.call-done = bf16[3584,512]{1,0:T(8,128)(2,1)} async-done(((bf16[112,512]{1,0:T(8,128)(2,1)}), bf16[3584,512]{1,0:T(8,128)(2,1)}) %all-gather.3.cloned.1.call-update) | async-done | bytes 3670032 | tf_op jit(solution)/shard_map/all_gather | solution.py:41
  321.8 4.5 convolution_convert_fusion
  326.3 28.5 %all-to-all-start.9 = ((bf16[32,8,3584]{2,1,0:T(8,128)(2,1)}), bf16[32,8,3584]{2,1,0:T(8,128)(2,1)}, u32[]{:S(2)}, u32[]{:S(2)}) async-start(bf16[32,8,3584]{2,1,0:T(8,128)(2,1)} %convolution_convert_fusion), calls=%async_computation.9 | async-start | bytes 3670016 | tf_op jit(solution)/shard_map/all_to_all | solution.py:61
  354.9 2.0 sort.59
  356.9 2.0 sort.60
  359.4 21.0 %all-to-all-done.9 = bf16[32,8,3584]{2,1,0:T(8,128)(2,1)} async-done(((bf16[32,8,3584]{2,1,0:T(8,128)(2,1)}), bf16[32,8,3584]{2,1,0:T(8,128)(2,1)}, u32[]{:S(2)}, u32[]{:S(2)}) %all-to-all-start.9) | async-done | bytes 1835040 | tf_op jit(solution)/shard_map/all_to_all | solution.py:61
  380.4 1.9 convert_reduce_fusion
  382.3 1.8 gather_fusion.3
  384.2 1.8 fusion.8
  385.9 2.4 fusion.20
  389.5 29.4 %all_to_all.55 = bf16[32,8,3584]{2,1,0:T(8,128)(2,1)S(1)} all-to-all(bf16[32,8,3584]{2,1,0:T(8,128)(2,1)S(1)} %bitcast.77), channel_id=1, replica_groups=mesh['x'=4,'zl'=8,'y'=4,'zh'=4,'c'=2] {'x','y','c'}, dimensions={0} | all-to-all | bytes 3670016 | tf_op jit(solution)/shard_map/all_to_all | solution.py:53
  420.4 1.9 convolution_convert_fusion.1
  422.3 4.5 all-to-all-start.5
  426.8 8.6 %collective-permute-start.1 = (bf16[1,64,3584]{2,1,0:T(8,128)(2,1)}, bf16[1,64,3584]{2,1,0:T(8,128)(2,1)}, u32[]{:S(2)}, u32[]{:S(2)}) collective-permute-start(bf16[1,64,3584]{2,1,0:T(8,128)(2,1)} %get-tuple-element.14), channel_id=1, source_target_pairs={{0,992},{32,0},{64,32},{96,64},{128,96},{160,128},{192,160},{224,1... | collective-permute-start | bytes 1376264 | tf_op jit(solution)/shard_map/ppermute | solution.py:70
  435.4 16.8 %all-to-all-done.5 = bf16[32,8,3584]{2,1,0:T(8,128)(2,1)} async-done(((bf16[32,8,3584]{2,1,0:T(8,128)(2,1)}), bf16[32,8,3584]{2,1,0:T(8,128)(2,1)}, u32[]{:S(2)}, u32[]{:S(2)}) %all-to-all-start.5) | async-done | bytes 1835040 | tf_op jit(solution)/shard_map/all_to_all | solution.py:61
  452.2 1.9 convert_reduce_fusion.1
  454.1 1.8 gather_fusion.1
  457.3 2.2 collective-permute-start
  459.5 22.8 %collective-permute-done = bf16[1,64,3584]{2,1,0:T(8,128)(2,1)S(1)} collective-permute-done((bf16[1,64,3584]{2,1,0:T(8,128)(2,1)S(1)}, bf16[1,64,3584]{2,1,0:T(8,128)(2,1)S(1)}, u32[]{:S(2)}, u32[]{:S(2)}) %collective-permute-start) | collective-permute-done | bytes 458784 | tf_op jit(solution)/shard_map/ppermute | solution.py:70
  483.1 1.8 copy.30
  (66 shorter events, 11.9 us)
Async XLA Ops:
  7.2 1.5 copy-start
  7.2 100.6 %copy-start.11 = (s32[1,64,1]{1,2,0:T(1,128)S(1)}, s32[1,64,1]{1,2,0:T(1,128)}, u32[]{:S(2)}) copy-start(s32[1,64,1]{1,2,0:T(1,128)} %param.19) | copy-start | bytes 772
  7.2 104.8 %copy-start.1 = (bf16[1,64,3584]{2,1,0:T(8,128)(2,1)S(1)}, bf16[1,64,3584]{2,1,0:T(8,128)(2,1)}, u32[]{:S(2)}) copy-start(bf16[1,64,3584]{2,1,0:T(8,128)(2,1)} %param.18) | copy-start | bytes 1376260
  7.2 182.6 %all-gather.5.cloned.1.call-start = ((), (), s32[]{:S(2)}) async-start(), calls=%async_computation.11 | async-start | bytes 1892352 | tf_op jit(solution)/shard_map/all_gather | solution.py:41
  67.8 254.0 %all-gather.3.cloned.1.call-start = ((), (), s32[]{:S(2)}) async-start(), calls=%async_computation.10 | async-start | bytes 3784704 | tf_op jit(solution)/shard_map/all_gather | solution.py:41
  103.7 32.9 %all-to-all-start.7 = ((bf16[4,64,512]{2,1,0:T(8,128)(2,1)}), bf16[4,64,512]{2,1,0:T(8,128)(2,1)}, u32[]{:S(2)}, u32[]{:S(2)}) async-start(bf16[4,64,512]{2,1,0:T(8,128)(2,1)} %bitcast.28), calls=%async_computation.7 | async-start | bytes 524288 | tf_op jit(solution)/shard_map/all_to_all | solution.py:25
  136.5 10.9 %all-to-all-start.8 = ((bf16[4,64,512]{2,1,0:T(8,128)(2,1)}), bf16[4,64,512]{2,1,0:T(8,128)(2,1)S(1)}, u32[]{:S(2)}, u32[]{:S(2)}) async-start(bf16[4,64,512]{2,1,0:T(8,128)(2,1)} %all-to-all-done.7), calls=%async_computation.8 | async-start | bytes 524288 | tf_op jit(solution)/shard_map/all_to_all | solution.py:26
  326.3 28.5 %copy-start.8 = (f32[1,3584]{1,0:T(1,128)S(1)}, f32[1,3584]{1,0:T(1,128)}, u32[]{:S(2)}) copy-start(f32[1,3584]{1,0:T(1,128)} %param.23) | copy-start | bytes 43012
  326.3 28.5 %copy-start.12 = (s32[1,64,1]{1,2,0:T(1,128)S(1)}, s32[1,64,1]{1,2,0:T(1,128)}, u32[]{:S(2)}) copy-start(s32[1,64,1]{1,2,0:T(1,128)} %param.16) | copy-start | bytes 772
  326.3 32.6 %copy-start.5 = (bf16[1,64,3584]{2,1,0:T(8,128)(2,1)S(1)}, bf16[1,64,3584]{2,1,0:T(8,128)(2,1)}, u32[]{:S(2)}) copy-start(bf16[1,64,3584]{2,1,0:T(8,128)(2,1)} %param.21) | copy-start | bytes 1376260
  326.3 32.9 %copy-start.3 = (bf16[1,64,3584]{2,1,0:T(8,128)(2,1)S(1)}, bf16[1,64,3584]{2,1,0:T(8,128)(2,1)}, u32[]{:S(2)}) copy-start(bf16[1,64,3584]{2,1,0:T(8,128)(2,1)} %param.15) | copy-start | bytes 1376260
  326.3 54.0 %all-to-all-start.9 = ((bf16[32,8,3584]{2,1,0:T(8,128)(2,1)}), bf16[32,8,3584]{2,1,0:T(8,128)(2,1)}, u32[]{:S(2)}, u32[]{:S(2)}) async-start(bf16[32,8,3584]{2,1,0:T(8,128)(2,1)} %convolution_convert_fusion), calls=%async_computation.9 | async-start | bytes 3670016 | tf_op jit(solution)/shard_map/all_to_all | solution.py:61
  382.3 1.8 copy-start.9
  384.2 1.8 copy-start.2
  389.5 29.4 %copy-start.6 = (bf16[3584,512]{1,0:T(8,128)(2,1)S(1)}, bf16[3584,512]{1,0:T(8,128)(2,1)}, u32[]{:S(2)}) copy-start(bf16[3584,512]{1,0:T(8,128)(2,1)} %all-gather.3.cloned.1.call-done) | copy-start | bytes 11010052
  418.9 1.5 copy-start.7
  422.3 29.9 %all-to-all-start.5 = ((bf16[32,8,3584]{2,1,0:T(8,128)(2,1)}), bf16[32,8,3584]{2,1,0:T(8,128)(2,1)}, u32[]{:S(2)}, u32[]{:S(2)}) async-start(bf16[32,8,3584]{2,1,0:T(8,128)(2,1)} %convolution_convert_fusion.1), calls=%async_computation.5 | async-start | bytes 3670016 | tf_op jit(solution)/shard_map/all_to_all | solution.py:61
  426.8 32.7 %collective-permute-start.1 = (bf16[1,64,3584]{2,1,0:T(8,128)(2,1)}, bf16[1,64,3584]{2,1,0:T(8,128)(2,1)}, u32[]{:S(2)}, u32[]{:S(2)}) collective-permute-start(bf16[1,64,3584]{2,1,0:T(8,128)(2,1)} %get-tuple-element.14), channel_id=1, source_target_pairs={{0,992},{32,0},{64,32},{96,64},{128,96},{160,128},{192,160},{224,1... | collective-permute-start | bytes 1376264 | tf_op jit(solution)/shard_map/ppermute | solution.py:70
  454.1 1.8 copy-start.4
  454.1 1.8 copy-start.10
  457.3 25.0 %collective-permute-start = (bf16[1,64,3584]{2,1,0:T(8,128)(2,1)S(1)}, bf16[1,64,3584]{2,1,0:T(8,128)(2,1)S(1)}, u32[]{:S(2)}, u32[]{:S(2)}) collective-permute-start(bf16[1,64,3584]{2,1,0:T(8,128)(2,1)S(1)} %fusion.19), channel_id=1, source_target_pairs={{0,32},{32,64},{64,96},{96,128},{128,160},{160,192},{192,224},{224... | collective-permute-start | bytes 1376264 | tf_op jit(solution)/shard_map/ppermute | solution.py:70
Sparse Core Ops, SparseCore 0:
  67.9 121.8 all-gather.4
  193.0 128.7 all-gather.2

commit v2 on v0

v2 whole, which is shorter than its diff:
```python
import jax
import jax.numpy as jnp
import numpy as np
from jax import lax
from jax.experimental import pallas as pl
from jax.experimental.pallas import tpu as pltpu
from jax.sharding import Mesh, PartitionSpec as P

epsilon = 1e-06
PIPE = ("x", "zj", "zp")
FAR = ("zh", "c")
NEAR = ("x", "zp")
GROUP = ("x", "zp", "y")
RING = ("zh", "zj", "c")


def normalize(tokens, norm_scale):
    widened = tokens.astype(jnp.float32)
    inverse_rms = lax.rsqrt(jnp.mean(widened * widened, axis=-1, keepdims=True) + epsilon)
    return (widened * inverse_rms * norm_scale).astype(jnp.bfloat16)


def selection(route_ids, experts, capacity):
    ids = route_ids[:, 0]
    tokens = ids.shape[0]
    row = lax.broadcasted_iota(jnp.int32, (tokens, tokens), 0)
    column = lax.broadcasted_iota(jnp.int32, (tokens, tokens), 1)
    earlier = (ids[:, None] == ids[None, :]) & (column < row)
    slot = ids * capacity + jnp.sum(earlier.astype(jnp.int32), axis=1)
    xs, zs, ys = lax.axis_size("x"), lax.axis_size("zp"), lax.axis_size("y")
    pairs = experts // ys
    x, _, y, rank = np.indices((xs, zs, ys, capacity))
    place = ((y * pairs + x // (xs // pairs)) * capacity + rank).reshape(1, -1)
    return (slot[:, None] == jnp.asarray(place, jnp.int32)).astype(jnp.bfloat16)


def exchanged(rows, axes):
    return lax.all_to_all(rows, axes, split_axis=0, concat_axis=0, tiled=True)


def weight_pieces(weight_in, weight_out):
    width, columns = weight_in.shape
    hidden = weight_out.shape[0]
    far, run, parts = lax.axis_size(FAR), lax.axis_size("zj"), lax.axis_size(RING)
    zh, cs = lax.axis_size("zh"), lax.axis_size("c")
    strips, halves = lax.axis_size("x"), lax.axis_size("zp")
    tall, wide = width // parts // halves, columns // strips
    deep = hidden // parts
    pieces = width // columns
    j, x, half = lax.axis_index("zj"), lax.axis_index("x"), lax.axis_index("zp")
    first = lax.dynamic_slice(
        weight_in.reshape(zh, run, cs, halves, tall, columns),
        (0, j, 0, half, 0, x * wide),
        (zh, 1, cs, 1, tall, wide),
    ).reshape(far, tall, wide)
    piece = jnp.minimum(x * halves + half, pieces - 1)
    second = lax.dynamic_slice(
        weight_out.reshape(zh, run, cs, deep, width),
        (0, j, 0, 0, piece * columns),
        (zh, 1, cs, deep, columns),
    )
    second = second.reshape(far, deep, strips, wide).transpose(0, 2, 1, 3)
    return jnp.concatenate([first, second.reshape(far, strips * deep, wide)], axis=1)


def expert_kernel(fwd_ref, grad_ref, acts_ref, parts_ref, fwd_out, grad_out, first_ref, second_ref, sems):
    parts, halves, tall, columns = first_ref.shape
    _, deep, width = second_ref.shape
    wide = parts_ref.shape[3]
    strips = columns // wide
    hidden = parts * deep
    first_copies = [
        pltpu.make_async_copy(
            parts_ref.at[:, s * halves + h, pl.ds(0, tall), :],
            first_ref.at[:, h, :, pl.ds(s * wide, wide)],
            sems.at[s * halves + h],
        )
        for s in range(strips)
        for h in range(halves)
    ]
    second_copies = [
        pltpu.make_async_copy(
            parts_ref.at[:, q // strips, pl.ds(tall + q % strips * deep, deep), :],
            second_ref.at[:, :, pl.ds(q * wide, wide)],
            sems.at[strips * halves + q],
        )
        for q in range(width // wide)
    ]
    for copy in first_copies + second_copies:
        copy.start()
    for copy in first_copies:
        copy.wait()
    first = first_ref[...].reshape(parts * halves * tall, columns)
    projected = jnp.dot(fwd_ref[...], first, preferred_element_type=jnp.float32)
    gate, up = projected[:, :hidden], projected[:, hidden:]
    mixed = (gate / (1.0 + jnp.exp(-gate)) * up).astype(jnp.bfloat16)
    for copy in second_copies:
        copy.wait()
    second = second_ref[...].reshape(hidden, width)
    fwd_out[...] = jnp.dot(mixed, second, preferred_element_type=jnp.float32).astype(jnp.bfloat16)
    turned = (((1,), (1,)), ((), ()))
    hidden_grad = lax.dot_general(grad_ref[...], second, turned, preferred_element_type=jnp.float32)
    gate_act = acts_ref[:, :hidden].astype(jnp.float32)
    up_act = acts_ref[:, hidden:].astype(jnp.float32)
    squashed = 1.0 / (1.0 + jnp.exp(-gate_act))
    gate_grad = hidden_grad * up_act * squashed * (1.0 + gate_act * (1.0 - squashed))
    up_grad = hidden_grad * gate_act * squashed
    joined = jnp.concatenate([gate_grad.astype(jnp.bfloat16), up_grad.astype(jnp.bfloat16)], axis=1)
    grad_out[...] = lax.dot_general(
        joined, first, turned, preferred_element_type=jnp.float32
    ).astype(jnp.bfloat16)


def experts_of(fwd_rows, grad_rows, acts, parts, halves, deep):
    count, pieces, height, wide = parts.shape
    rows, width = fwd_rows.shape
    columns = acts.shape[1]
    tall = width // count // halves
    vmem, hbm = pl.BlockSpec(memory_space=pltpu.VMEM), pl.BlockSpec(memory_space=pl.ANY)
    out = jax.ShapeDtypeStruct((rows, width), jnp.bfloat16)
    return pl.pallas_call(
        expert_kernel,
        out_shape=(out, out),
        in_specs=[vmem, vmem, vmem, hbm],
        out_specs=(vmem, vmem),
        scratch_shapes=[
            pltpu.VMEM((count, halves, tall, columns), jnp.bfloat16),
            pltpu.VMEM((count, deep, width), jnp.bfloat16),
            pltpu.SemaphoreType.DMA((pieces + width // wide,)),
        ],
        compiler_params=pltpu.CompilerParams(vmem_limit_bytes=40 * 1024 * 1024),
        cost_estimate=pl.CostEstimate(
            flops=12 * rows * width * count * deep,
            bytes_accessed=count * pieces * height * wide * 2,
            transcendentals=2 * rows * count * deep,
        ),
        name="experts",
    )(fwd_rows, grad_rows, acts, parts)


def shifted(array, by):
    sections = lax.axis_size(PIPE)
    return lax.ppermute(array, PIPE, [(i, (i + by) % sections) for i in range(sections)])


def picked(chosen, rows, axis):
    return lax.dot_general(
        chosen, rows, (((axis,), (0,)), ((), ())), preferred_element_type=jnp.float32
    )


def on_device(
    forward_in,
    forward_ids,
    forward_gates,
    grad_in,
    grad_ids,
    grad_gates,
    saved_input,
    saved_acts,
    norm_gain,
    weight_in,
    weight_out,
):
    tokens, grads, norm_scale = forward_in[0], grad_in[0], norm_gain[0]
    token_count, model_width = tokens.shape
    experts = lax.axis_size(("y", "zh", "c")) // 4
    capacity = token_count // experts
    hidden, columns = weight_out.shape[1], weight_in.shape[2]
    places = lax.axis_size(GROUP)

    got = exchanged(weight_pieces(weight_in[0], weight_out[0]), FAR)
    grad_chosen = selection(grad_ids[0], experts, capacity)
    grad_sent = picked(grad_chosen, grads, 0).astype(jnp.bfloat16)
    grad_rows = exchanged(grad_sent.reshape(places, capacity, model_width), GROUP)
    part = exchanged(got, NEAR)
    parts = lax.all_gather(part, RING, axis=0)

    fwd_chosen = selection(forward_ids[0], experts, capacity)
    fwd_sent = picked(fwd_chosen, normalize(tokens, norm_scale), 0).astype(jnp.bfloat16)
    fwd_rows = exchanged(fwd_sent.reshape(places, capacity, model_width), GROUP)
    ys, far = lax.axis_size("y"), lax.axis_size(FAR)
    acts = saved_acts[0, 0].reshape(ys, far, capacity, columns).transpose(1, 0, 2, 3)
    acts = exchanged(acts.reshape(far, ys * capacity, columns), FAR)
    acts = exchanged(acts, NEAR)

    rows = places * capacity
    fwd_part, grad_part = experts_of(
        fwd_rows.reshape(rows, model_width),
        grad_rows.reshape(rows, model_width),
        acts.reshape(rows, columns),
        parts,
        lax.axis_size("zp"),
        hidden // lax.axis_size(RING),
    )
    fwd_back = exchanged(fwd_part.reshape(places, capacity, model_width), GROUP)
    grad_back = exchanged(grad_part.reshape(places, capacity, model_width), GROUP)

    combined = forward_gates[0] * picked(fwd_chosen, fwd_back.reshape(rows, model_width), 1)
    moved = (tokens.astype(jnp.float32) + combined).astype(jnp.bfloat16)
    pulled = grad_gates[0] * picked(grad_chosen, grad_back.reshape(rows, model_width), 1)
    widened = saved_input[0].astype(jnp.float32)
    inverse_rms = lax.rsqrt(jnp.mean(widened * widened, axis=-1, keepdims=True) + epsilon)
    unit_rows = widened * inverse_rms
    weighted = pulled * norm_scale
    through = grads.astype(jnp.float32) + inverse_rms * (
        weighted - unit_rows * jnp.mean(weighted * unit_rows, axis=-1, keepdims=True)
    )
    return (shifted(moved[None], 1), shifted(through.astype(jnp.bfloat16)[None], -1))


def solution(mesh):
    fine = Mesh(mesh.devices.reshape(4, 4, 2, 4, 4, 2), ("x", "zj", "zp", "y", "zh", "c"))
    expert = ("y", "zh", "c")
    rows = P(PIPE, expert, None)
    placed = (rows,) * 7 + (
        P(PIPE, expert, None, None),
        P(PIPE, None),
        P(expert, None, None),
        P(expert, None, None),
    )
    return jax.shard_map(
        on_device, mesh=fine, in_specs=placed, out_specs=(rows, rows), check_vma=False
    )
```

time: 801 us -> 385 us (0.48)
  blocking collectives: 379 us -> 93.2 us
  waiting for transfers between devices: 327 us -> 183 us
  other arithmetic: 18.9 us -> 2.56 us
  starting transfers between devices: 46.9 us -> 62 us
  between operations: 0.93 us -> 14.3 us
    all_to_all x2 -> x3, blocking collectives: 379 us -> 93.2 us  [exchanged(): return lax.all_to_all(rows, axes, split_axis=0, concat_axis=0, tiled=True)]
    all_to_all x2 -> x5, waiting for transfers between devices: 268 us -> 62 us  [exchanged(): return lax.all_to_all(rows, axes, split_axis=0, concat_axis=0, tiled=True)]
    all_gather x0 -> x1, waiting for transfers between devices: none -> 104 us  [on_device(): parts = lax.all_gather(part, RING, axis=0)]
    ppermute x2, waiting for transfers between devices: 59.4 us -> 16.1 us  [shifted(): lax.ppermute(array, PIPE, [(i, (i + by) % sections) for i in range(sectio...]
    all_to_all x2 -> x5, starting transfers between devices: 30 us -> 49.4 us  [exchanged(): return lax.all_to_all(rows, axes, split_axis=0, concat_axis=0, tiled=True)]
    sort x4 -> x0, other arithmetic: 8.92 us -> none  [the longest x2 4.85 us: slot_order(): sorted_pairs = jnp.argsort(flattened, stable=True)]
  transfers between devices with their start and end apart: 4 -> 8, of which waited for: 4 -> 7; matrix products, arithmetic and copies ran while one was open for 1% -> 3% of each run, Pallas kernels for 0% -> 0%
where the time goes in v2:
time: 385 us; the launch traced here: 379 us
  waiting for transfers between devices  183 us (48%)
  blocking collectives  93.2 us (24%)
  starting transfers between devices  62 us (16%)
  between operations  14.3 us (4%)
  matrix products  8.13 us (2%)
  Pallas kernels  7.78 us (2%)
  local copies, waits for them, and re-layouts  7.72 us (2%)
    all_gather x1, waiting for transfers between devices, on_device(): parts = lax.all_gather(part, RING, axis=0)  104 us
    all_to_all x3, blocking collectives, exchanged(): return lax.all_to_all(rows, axes, split_axis=0, concat_axis=0, tiled=True)  93.2 us
    all_to_all x5, waiting for transfers between devices, exchanged(): return lax.all_to_all(rows, axes, split_axis=0, concat_axis=0, tiled=True)  62 us
    all_to_all x5, starting transfers between devices, exchanged(): return lax.all_to_all(rows, axes, split_axis=0, concat_axis=0, tiled=True)  49.4 us
    ppermute x2, waiting for transfers between devices, shifted(): lax.ppermute(array, PIPE, [(i, (i + by) % sections) for i in range(sectio...  16.1 us
    ppermute x2, starting transfers between devices, shifted(): lax.ppermute(array, PIPE, [(i, (i + by) % sections) for i in range(sectio...  12.6 us
    dot_general x4, matrix products, picked(): lax.dot_general(chosen, rows, (((axis,), (0,)), ((), ())), preferred_elem...  8.13 us
    pallas_call x1, Pallas kernels, experts_of(): pl.pallas_call(expert_kernel, out_shape=(out, out), in_specs=[vmem, vmem,...  7.78 us
  transfers between devices with their start and end apart: 8, of which 7 were waited for; matrix products, arithmetic and copies ran while one was open for 3% of the time, Pallas kernels for 0%

profile of v2, /device:TPU:1, one launch (start us, length us, event | category | flops | bytes accessed | tf_op | source)
XLA Modules:
  0.0 378.8 jit_solution(9400982583170019018)
XLA Ops:
  7.2 1.6 copy-done
  8.8 0.9 constant_dynamic-slice_fusion.1
  9.8 0.7 pad_maximum_fusion
  10.5 29.8 %all-to-all-start.4 = ((bf16[8,88,128]{2,1,0:T(8,128)(2,1)}), bf16[8,88,128]{2,1,0:T(8,128)(2,1)S(1)}, u32[]{:S(2)}, u32[]{:S(2)}) async-start(bf16[8,88,128]{2,1,0:T(8,128)(2,1)} %pad_maximum_fusion), calls=%async_computation.4 | async-start | bytes 360448 | tf_op jit(solution)/shard_map/all_to_all | solution.py:38
  40.3 1.0 copy.22
  41.3 28.4 %all-to-all-done.4 = bf16[8,88,128]{2,1,0:T(8,128)(2,1)S(1)} async-done(((bf16[8,88,128]{2,1,0:T(8,128)(2,1)}), bf16[8,88,128]{2,1,0:T(8,128)(2,1)S(1)}, u32[]{:S(2)}, u32[]{:S(2)}) %all-to-all-start.4) | async-done | bytes 180256 | tf_op jit(solution)/shard_map/all_to_all | solution.py:38
  69.6 42.7 %all_to_all.40 = bf16[8,32,512]{2,1,0:T(8,128)(2,1)} all-to-all(bf16[8,32,512]{2,1,0:T(8,128)(2,1)S(1)} %bitcast.66), channel_id=1, replica_groups=mesh['x'=4,'zj'=4,'zp'=2,'y'=4,'zh'=4,'c'=2] {'zh','c'}, dimensions={0} | all-to-all | bytes 524288 | tf_op jit(solution)/shard_map/all_to_all | solution.py:38
  112.3 18.8 %all_to_all.41 = bf16[8,88,128]{2,1,0:T(8,128)(2,1)} all-to-all(bf16[8,88,128]{2,1,0:T(8,128)(2,1)S(1)} %all-to-all-done.4), channel_id=1, replica_groups=mesh['x'=4,'zj'=4,'zp'=2,'y'=4,'zh'=4,'c'=2] {'x','zp'}, dimensions={0} | all-to-all | bytes 360448 | tf_op jit(solution)/shard_map/all_to_all | solution.py:38
  131.1 3.4 all-to-all-start.3
  134.8 0.2 fusion.16
  135.0 2.1 fusion
  137.1 3.5 all-to-all-done.3
  140.6 5.9 %all-to-all-start = ((bf16[32,8,3584]{2,1,0:T(8,128)(2,1)}), bf16[32,8,3584]{2,1,0:T(8,128)(2,1)}, u32[]{:S(2)}, u32[]{:S(2)}) async-start(bf16[32,8,3584]{2,1,0:T(8,128)(2,1)} %fusion), calls=%async_computation | async-start | bytes 3670016 | tf_op jit(solution)/shard_map/all_to_all | solution.py:38
  146.8 2.0 fusion.1
  148.7 19.8 %all-to-all-done = bf16[32,8,3584]{2,1,0:T(8,128)(2,1)} async-done(((bf16[32,8,3584]{2,1,0:T(8,128)(2,1)}), bf16[32,8,3584]{2,1,0:T(8,128)(2,1)}, u32[]{:S(2)}, u32[]{:S(2)}) %all-to-all-start) | async-done | bytes 1835040 | tf_op jit(solution)/shard_map/all_to_all | solution.py:38
  168.6 5.4 %all-to-all-start.1 = ((bf16[32,8,3584]{2,1,0:T(8,128)(2,1)}), bf16[32,8,3584]{2,1,0:T(8,128)(2,1)}, u32[]{:S(2)}, u32[]{:S(2)}) async-start(bf16[32,8,3584]{2,1,0:T(8,128)(2,1)} %fusion.1), calls=%async_computation.1 | async-start | bytes 3670016 | tf_op jit(solution)/shard_map/all_to_all | solution.py:38
  174.0 0.7 all-gather.3.cloned.1.call-update
  174.7 104.4 %all-gather.3.cloned.1.call-done = bf16[256,88,128]{2,1,0:T(8,128)(2,1)} async-done(((bf16[8,88,128]{2,1,0:T(8,128)(2,1)}), bf16[256,88,128]{2,1,0:T(8,128)(2,1)}) %all-gather.3.cloned.1.call-update) | async-done | bytes 5767184 | tf_op jit(solution)/shard_map/all_gather | solution.py:177
  279.1 2.6 copy-done.2
  281.7 7.8 %experts.1 = (bf16[256,3584]{1,0:T(8,128)(2,1)S(1)}, bf16[256,3584]{1,0:T(8,128)(2,1)S(1)}) custom-call(bf16[256,3584]{1,0:T(8,128)(2,1)} %bitcast.5.fwd_ref, bf16[256,3584]{1,0:T(8,128)(2,1)} %bitcast.9.grad_ref, bf16[256,512]{1,0:T(8,128)(2,1)S(1)} %bitcast.64, bf16[32,8,88,128]{3,2,1,0:T(8,128)(2,1)S(1)} %bitcast.65), custom_call_target="tpu_custom_call" | custom-call | flops 2818572288 | bytes 5767168 | tf_op jit(solution)/shard_map/experts/pallas_call | solution.py:121
  289.5 31.7 %all_to_all.42 = bf16[32,8,3584]{2,1,0:T(8,128)(2,1)} all-to-all(bf16[32,8,3584]{2,1,0:T(8,128)(2,1)S(1)} %bitcast.63), channel_id=1, replica_groups=mesh['x'=4,'zj'=4,'zp'=2,'y'=4,'zh'=4,'c'=2] {'x','zp','y'}, dimensions={0} | all-to-all | bytes 3670016 | tf_op jit(solution)/shard_map/all_to_all | solution.py:38
  321.2 4.9 %all-to-all-start.6 = ((bf16[32,8,3584]{2,1,0:T(8,128)(2,1)}), bf16[32,8,3584]{2,1,0:T(8,128)(2,1)}, u32[]{:S(2)}, u32[]{:S(2)}) async-start(bf16[32,8,3584]{2,1,0:T(8,128)(2,1)} %bitcast.62), calls=%async_computation.6 | async-start | bytes 3670016 | tf_op jit(solution)/shard_map/all_to_all | solution.py:38
  326.3 2.1 fusion.10
  328.4 1.1 fusion.20
  329.5 10.6 %collective-permute-start.1 = (bf16[1,64,3584]{2,1,0:T(8,128)(2,1)}, bf16[1,64,3584]{2,1,0:T(8,128)(2,1)S(1)}, u32[]{:S(2)}, u32[]{:S(2)}) collective-permute-start(bf16[1,64,3584]{2,1,0:T(8,128)(2,1)} %fusion.20), channel_id=1, source_target_pairs={{0,992},{32,0},{64,32},{96,64},{128,96},{160,128},{192,160},{224,1... | collective-permute-start | bytes 1376264 | tf_op jit(solution)/shard_map/ppermute | solution.py:143
  340.1 10.3 %all-to-all-done.6 = bf16[32,8,3584]{2,1,0:T(8,128)(2,1)} async-done(((bf16[32,8,3584]{2,1,0:T(8,128)(2,1)}), bf16[32,8,3584]{2,1,0:T(8,128)(2,1)}, u32[]{:S(2)}, u32[]{:S(2)}) %all-to-all-start.6) | async-done | bytes 1835040 | tf_op jit(solution)/shard_map/all_to_all | solution.py:38
  350.4 2.0 fusion.5
  352.4 1.9 collective-permute-start
  354.3 1.5 collective-permute-done.1
  355.9 14.5 %collective-permute-done = bf16[1,64,3584]{2,1,0:T(8,128)(2,1)S(1)} collective-permute-done((bf16[1,64,3584]{2,1,0:T(8,128)(2,1)S(1)}, bf16[1,64,3584]{2,1,0:T(8,128)(2,1)S(1)}, u32[]{:S(2)}, u32[]{:S(2)}) %collective-permute-start) | collective-permute-done | bytes 458784 | tf_op jit(solution)/shard_map/ppermute | solution.py:143
  370.4 0.8 copy.25
  371.2 0.8 copy.26
  (34 shorter events, 0.7 us)
Async XLA Ops:
  7.2 1.7 copy-start
  7.2 127.8 %copy-start.6 = (s32[256]{0:T(256)S(1)}, s32[256]{0:T(256)}, u32[]{:S(2)}) copy-start(s32[256]{0:T(256)} %constant.55) | copy-start | bytes 3076
  7.2 127.4 %copy-start.7 = (f32[1,3584]{1,0:T(1,128)S(1)}, f32[1,3584]{1,0:T(1,128)}, u32[]{:S(2)}) copy-start(f32[1,3584]{1,0:T(1,128)} %param.21) | copy-start | bytes 43012
  7.2 127.4 %copy-start.10 = (s32[1,64,1]{1,2,0:T(1,128)S(1)}, s32[1,64,1]{1,2,0:T(1,128)}, u32[]{:S(2)}) copy-start(s32[1,64,1]{1,2,0:T(1,128)} %param.14) | copy-start | bytes 772
  7.2 127.6 %copy-start.3 = (bf16[1,64,3584]{2,1,0:T(8,128)(2,1)S(1)}, bf16[1,64,3584]{2,1,0:T(8,128)(2,1)}, u32[]{:S(2)}) copy-start(bf16[1,64,3584]{2,1,0:T(8,128)(2,1)} %param.13) | copy-start | bytes 1376260
  10.5 59.2 %all-to-all-start.4 = ((bf16[8,88,128]{2,1,0:T(8,128)(2,1)}), bf16[8,88,128]{2,1,0:T(8,128)(2,1)S(1)}, u32[]{:S(2)}, u32[]{:S(2)}) async-start(bf16[8,88,128]{2,1,0:T(8,128)(2,1)} %pad_maximum_fusion), calls=%async_computation.4 | async-start | bytes 360448 | tf_op jit(solution)/shard_map/all_to_all | solution.py:38
  131.1 9.5 %all-to-all-start.3 = ((bf16[8,32,512]{2,1,0:T(8,128)(2,1)}), bf16[8,32,512]{2,1,0:T(8,128)(2,1)S(1)}, u32[]{:S(2)}, u32[]{:S(2)}) async-start(bf16[8,32,512]{2,1,0:T(8,128)(2,1)} %all_to_all.40), calls=%async_computation.3 | async-start | bytes 524288 | tf_op jit(solution)/shard_map/all_to_all | solution.py:38
  137.1 9.5 %copy-start.11 = (s32[1,64,1]{1,2,0:T(1,128)S(1)}, s32[1,64,1]{1,2,0:T(1,128)}, u32[]{:S(2)}) copy-start(s32[1,64,1]{1,2,0:T(1,128)} %param.17) | copy-start | bytes 772
  137.1 9.7 %copy-start.5 = (bf16[1,64,3584]{2,1,0:T(8,128)(2,1)S(1)}, bf16[1,64,3584]{2,1,0:T(8,128)(2,1)}, u32[]{:S(2)}) copy-start(bf16[1,64,3584]{2,1,0:T(8,128)(2,1)} %param.16) | copy-start | bytes 1376260
  140.6 27.9 %all-to-all-start = ((bf16[32,8,3584]{2,1,0:T(8,128)(2,1)}), bf16[32,8,3584]{2,1,0:T(8,128)(2,1)}, u32[]{:S(2)}, u32[]{:S(2)}) async-start(bf16[32,8,3584]{2,1,0:T(8,128)(2,1)} %fusion), calls=%async_computation | async-start | bytes 3670016 | tf_op jit(solution)/shard_map/all_to_all | solution.py:38
  168.6 110.5 %all-to-all-start.1 = ((bf16[32,8,3584]{2,1,0:T(8,128)(2,1)}), bf16[32,8,3584]{2,1,0:T(8,128)(2,1)}, u32[]{:S(2)}, u32[]{:S(2)}) async-start(bf16[32,8,3584]{2,1,0:T(8,128)(2,1)} %fusion.1), calls=%async_computation.1 | async-start | bytes 3670016 | tf_op jit(solution)/shard_map/all_to_all | solution.py:38
  173.9 105.2 %all-gather.3.cloned.1.call-start = ((), (), s32[]{:S(2)}) async-start(), calls=%async_computation.8 | async-start | bytes 5947392 | tf_op jit(solution)/shard_map/all_gather | solution.py:177
  279.1 2.6 copy-start.2
  289.5 31.7 %copy-start.1 = (bf16[256,3584]{1,0:T(8,128)(2,1)}, bf16[256,3584]{1,0:T(8,128)(2,1)S(1)}, u32[]{:S(2)}) copy-start(bf16[256,3584]{1,0:T(8,128)(2,1)S(1)} %get-tuple-element.4) | copy-start | bytes 5505028
  321.2 4.9 %copy-start.4 = (bf16[1,64,3584]{2,1,0:T(8,128)(2,1)S(1)}, bf16[1,64,3584]{2,1,0:T(8,128)(2,1)}, u32[]{:S(2)}) copy-start(bf16[1,64,3584]{2,1,0:T(8,128)(2,1)} %param.19) | copy-start | bytes 1376260
  321.2 5.1 %copy-start.9 = (f32[1,64,1]{1,2,0:T(1,128)S(1)}, f32[1,64,1]{1,2,0:T(1,128)}, u32[]{:S(2)}) copy-start(f32[1,64,1]{1,2,0:T(1,128)} %param.18) | copy-start | bytes 772
  321.2 29.2 %all-to-all-start.6 = ((bf16[32,8,3584]{2,1,0:T(8,128)(2,1)}), bf16[32,8,3584]{2,1,0:T(8,128)(2,1)}, u32[]{:S(2)}, u32[]{:S(2)}) async-start(bf16[32,8,3584]{2,1,0:T(8,128)(2,1)} %bitcast.62), calls=%async_computation.6 | async-start | bytes 3670016 | tf_op jit(solution)/shard_map/all_to_all | solution.py:38
  328.4 22.0 %copy-start.8 = (f32[1,64,1]{1,2,0:T(1,128)S(1)}, f32[1,64,1]{1,2,0:T(1,128)}, u32[]{:S(2)}) copy-start(f32[1,64,1]{1,2,0:T(1,128)} %param.15) | copy-start | bytes 772
  329.5 26.4 %collective-permute-start.1 = (bf16[1,64,3584]{2,1,0:T(8,128)(2,1)}, bf16[1,64,3584]{2,1,0:T(8,128)(2,1)S(1)}, u32[]{:S(2)}, u32[]{:S(2)}) collective-permute-start(bf16[1,64,3584]{2,1,0:T(8,128)(2,1)} %fusion.20), channel_id=1, source_target_pairs={{0,992},{32,0},{64,32},{96,64},{128,96},{160,128},{192,160},{224,1... | collective-permute-start | bytes 1376264 | tf_op jit(solution)/shard_map/ppermute | solution.py:143
  352.4 18.0 %collective-permute-start = (bf16[1,64,3584]{2,1,0:T(8,128)(2,1)S(1)}, bf16[1,64,3584]{2,1,0:T(8,128)(2,1)S(1)}, u32[]{:S(2)}, u32[]{:S(2)}) collective-permute-start(bf16[1,64,3584]{2,1,0:T(8,128)(2,1)S(1)} %fusion.5), channel_id=1, source_target_pairs={{0,32},{32,64},{64,96},{96,128},{128,160},{160,192},{192,224},{224... | collective-permute-start | bytes 1376264 | tf_op jit(solution)/shard_map/ppermute | solution.py:143
Sparse Core Ops, SparseCore 0:
  177.5 101.5 all-gather.2

commit v3 on v2

v3 whole, which is shorter than its diff:
```python
import jax
import jax.numpy as jnp
import numpy as np
from jax import lax
from jax.experimental import pallas as pl
from jax.experimental.pallas import tpu as pltpu
from jax.sharding import Mesh, PartitionSpec as P

epsilon = 1e-06
PIPE = ("x", "zj", "zp")
FAR = ("zh", "c")
NEAR = ("x", "zp")
PLANE = ("x", "y")
BACK = ("x", "y", "zp")
RING = ("zh", "zj", "c")


def normalize(tokens, norm_scale):
    widened = tokens.astype(jnp.float32)
    inverse_rms = lax.rsqrt(jnp.mean(widened * widened, axis=-1, keepdims=True) + epsilon)
    return (widened * inverse_rms * norm_scale).astype(jnp.bfloat16)


def slots(route_ids, capacity):
    ids = route_ids[:, 0]
    tokens = ids.shape[0]
    row = lax.broadcasted_iota(jnp.int32, (tokens, tokens), 0)
    column = lax.broadcasted_iota(jnp.int32, (tokens, tokens), 1)
    earlier = (ids[:, None] == ids[None, :]) & (column < row)
    return ids * capacity + jnp.sum(earlier.astype(jnp.int32), axis=1)


def grouped(slot, rows):
    chosen = slot[:, None] == lax.broadcasted_iota(jnp.int32, (rows.shape[0],) * 2, 1)
    return picked(chosen.astype(jnp.bfloat16), rows, 0).astype(jnp.bfloat16)


def returned(slot, rows, experts, capacity):
    xs, ys, zs = lax.axis_size("x"), lax.axis_size("y"), lax.axis_size("zp")
    pairs = experts // ys
    x, y, _, rank = np.indices((xs, ys, zs, capacity))
    place = ((y * pairs + x // (xs // pairs)) * capacity + rank).reshape(1, -1)
    chosen = slot[:, None] == jnp.asarray(place, jnp.int32)
    return picked(chosen.astype(jnp.bfloat16), rows, 1)


def swapped_rows(rows):
    zs = lax.axis_size("zp")
    return lax.ppermute(rows, "zp", [(i, zs - 1 - i) for i in range(zs)])


def for_plane(own, partner, experts, capacity):
    xs, ys, zs = lax.axis_size("x"), lax.axis_size("y"), lax.axis_size("zp")
    pairs = experts // ys
    width = own.shape[1]
    even = lax.axis_index("zp") == 0
    both = jnp.stack([jnp.where(even, own, partner), jnp.where(even, partner, own)])
    both = both.reshape(zs, ys, pairs, capacity, width).transpose(2, 1, 0, 3, 4)
    both = jnp.broadcast_to(both[:, None], (pairs, xs // pairs, ys, zs, capacity, width))
    return both.reshape(xs * ys, zs * capacity, width)


def exchanged(rows, axes):
    return lax.all_to_all(rows, axes, split_axis=0, concat_axis=0, tiled=True)


def weight_pieces(weight_in, weight_out):
    width, columns = weight_in.shape
    hidden = weight_out.shape[0]
    far, run, parts = lax.axis_size(FAR), lax.axis_size("zj"), lax.axis_size(RING)
    zh, cs = lax.axis_size("zh"), lax.axis_size("c")
    strips, halves = lax.axis_size("x"), lax.axis_size("zp")
    tall, wide = width // parts // halves, columns // strips
    deep = hidden // parts
    pieces = width // columns
    j, x, half = lax.axis_index("zj"), lax.axis_index("x"), lax.axis_index("zp")
    first = lax.dynamic_slice(
        weight_in.reshape(zh, run, cs, halves, tall, columns),
        (0, j, 0, half, 0, x * wide),
        (zh, 1, cs, 1, tall, wide),
    ).reshape(far, tall, wide)
    piece = jnp.minimum(x * halves + half, pieces - 1)
    second = lax.dynamic_slice(
        weight_out.reshape(zh, run, cs, deep, width),
        (0, j, 0, 0, piece * columns),
        (zh, 1, cs, deep, columns),
    )
    second = second.reshape(far, deep, strips, wide).transpose(0, 2, 1, 3)
    return jnp.concatenate([first, second.reshape(far, strips * deep, wide)], axis=1)


def weight_copies(parts_ref, first_ref, second_ref, sems):
    _, halves, tall, columns = first_ref.shape
    _, deep, width = second_ref.shape
    wide = parts_ref.shape[3]
    strips = columns // wide
    first_copies = [
        pltpu.make_async_copy(
            parts_ref.at[:, s * halves + h, pl.ds(0, tall), :],
            first_ref.at[:, h, :, pl.ds(s * wide, wide)],
            sems.at[1 + s * halves + h],
        )
        for s in range(strips)
        for h in range(halves)
    ]
    second_copies = [
        pltpu.make_async_copy(
            parts_ref.at[:, q // strips, pl.ds(tall + q % strips * deep, deep), :],
            second_ref.at[:, :, pl.ds(q * wide, wide)],
            sems.at[1 + strips * halves + q],
        )
        for q in range(width // wide)
    ]
    return first_copies, second_copies


def forward_kernel(rows_hbm, parts_ref, out_ref, rows_ref, first_ref, second_ref, sems):
    parts, halves, tall, columns = first_ref.shape
    _, deep, width = second_ref.shape
    hidden = parts * deep
    first_copies, second_copies = weight_copies(parts_ref, first_ref, second_ref, sems)
    rows_copy = pltpu.make_async_copy(rows_hbm, rows_ref, sems.at[0])
    for copy in [rows_copy] + first_copies + second_copies:
        copy.start()
    for copy in [rows_copy] + first_copies:
        copy.wait()
    first = first_ref[...].reshape(parts * halves * tall, columns)
    projected = jnp.dot(rows_ref[...], first, preferred_element_type=jnp.float32)
    gate, up = projected[:, :hidden], projected[:, hidden:]
    mixed = (gate / (1.0 + jnp.exp(-gate)) * up).astype(jnp.bfloat16)
    for copy in second_copies:
        copy.wait()
    second = second_ref[...].reshape(hidden, width)
    out_ref[...] = jnp.dot(mixed, second, preferred_element_type=jnp.float32).astype(jnp.bfloat16)


def gradient_kernel(rows_hbm, parts_ref, acts_ref, out_ref, rows_ref, first_ref, second_ref, sems):
    parts, halves, tall, columns = first_ref.shape
    _, deep, width = second_ref.shape
    hidden = parts * deep
    first_copies, second_copies = weight_copies(parts_ref, first_ref, second_ref, sems)
    rows_copy = pltpu.make_async_copy(rows_hbm, rows_ref, sems.at[0])
    for copy in [rows_copy] + second_copies + first_copies:
        copy.start()
    for copy in [rows_copy] + second_copies:
        copy.wait()
    turned = (((1,), (1,)), ((), ()))
    second = second_ref[...].reshape(hidden, width)
    hidden_grad = lax.dot_general(rows_ref[...], second, turned, preferred_element_type=jnp.float32)
    gate_act = acts_ref[:, :hidden].astype(jnp.float32)
    up_act = acts_ref[:, hidden:].astype(jnp.float32)
    squashed = 1.0 / (1.0 + jnp.exp(-gate_act))
    gate_grad = hidden_grad * up_act * squashed * (1.0 + gate_act * (1.0 - squashed))
    up_grad = hidden_grad * gate_act * squashed
    joined = jnp.concatenate([gate_grad.astype(jnp.bfloat16), up_grad.astype(jnp.bfloat16)], axis=1)
    for copy in first_copies:
        copy.wait()
    first = first_ref[...].reshape(parts * halves * tall, columns)
    out_ref[...] = lax.dot_general(
        joined, first, turned, preferred_element_type=jnp.float32
    ).astype(jnp.bfloat16)


def experts_of(kernel, rows, parts, halves, hidden, *more):
    count, pieces, height, wide = parts.shape
    height_rows, width = rows.shape
    columns = 2 * hidden
    deep, tall = hidden // count, width // count // halves
    vmem, hbm = pl.BlockSpec(memory_space=pltpu.VMEM), pl.BlockSpec(memory_space=pl.ANY)
    return pl.pallas_call(
        kernel,
        out_shape=jax.ShapeDtypeStruct((height_rows, width), jnp.bfloat16),
        in_specs=[hbm, hbm] + [vmem] * len(more),
        out_specs=vmem,
        scratch_shapes=[
            pltpu.VMEM((height_rows, width), jnp.bfloat16),
            pltpu.VMEM((count, halves, tall, columns), jnp.bfloat16),
            pltpu.VMEM((count, deep, width), jnp.bfloat16),
            pltpu.SemaphoreType.DMA((1 + pieces + width // wide,)),
        ],
        compiler_params=pltpu.CompilerParams(vmem_limit_bytes=32 * 1024 * 1024),
        cost_estimate=pl.CostEstimate(
            flops=6 * height_rows * width * hidden,
            bytes_accessed=count * pieces * height * wide * 2,
            transcendentals=height_rows * hidden,
        ),
    )(rows, parts, *more)


def shifted(array, by):
    sections = lax.axis_size(PIPE)
    return lax.ppermute(array, PIPE, [(i, (i + by) % sections) for i in range(sections)])


def picked(chosen, rows, axis):
    return lax.dot_general(
        chosen, rows, (((axis,), (0,)), ((), ())), preferred_element_type=jnp.float32
    )


def on_device(
    forward_in,
    forward_ids,
    forward_gates,
    grad_in,
    grad_ids,
    grad_gates,
    saved_input,
    saved_acts,
    norm_gain,
    weight_in,
    weight_out,
):
    grads, norm_scale = grad_in[0], norm_gain[0]
    token_count, model_width = grads.shape
    experts = lax.axis_size(("y", "zh", "c")) // 4
    capacity = token_count // experts
    hidden, columns = weight_out.shape[1], weight_in.shape[2]
    halves, places = lax.axis_size("zp"), lax.axis_size(BACK)
    rows = places * capacity

    got = exchanged(weight_pieces(weight_in[0], weight_out[0]), FAR)
    part = exchanged(got, NEAR)
    parts = lax.all_gather(part, RING, axis=0)

    grad_slot = slots(grad_ids[0], capacity)
    grad_own = grouped(grad_slot, grads)
    grad_partner = swapped_rows(grad_own)

    small = jnp.concatenate(
        [norm_scale, forward_ids[0, :, 0].astype(jnp.float32), forward_gates[0, :, 0]]
    )
    tokens = shifted(forward_in, 1)[0]
    small = shifted(small[None], 1)[0]
    fwd_scale = small[:model_width]
    fwd_ids = small[model_width : model_width + token_count].astype(jnp.int32)
    fwd_gates = small[model_width + token_count :]
    fwd_slot = slots(fwd_ids[:, None], capacity)
    fwd_own = grouped(fwd_slot, normalize(tokens, fwd_scale))
    fwd_partner = swapped_rows(fwd_own)

    xs, zs, ys, far = lax.axis_size("x"), lax.axis_size("zp"), lax.axis_size("y"), lax.axis_size(FAR)
    acts = saved_acts[0, 0].reshape(ys, far, capacity, columns).transpose(1, 0, 2, 3)
    acts = exchanged(acts.reshape(far, ys * capacity, columns), FAR)
    acts = exchanged(acts, NEAR)
    acts = acts.reshape(xs, zs, ys, capacity, columns).transpose(0, 2, 1, 3, 4)

    grad_sent = for_plane(grad_own, grad_partner, experts, capacity)
    grad_rows = exchanged(grad_sent, PLANE).reshape(rows, model_width)
    fwd_sent = for_plane(fwd_own, fwd_partner, experts, capacity)
    fwd_rows = exchanged(fwd_sent, PLANE).reshape(rows, model_width)

    grad_part = experts_of(
        gradient_kernel, grad_rows, parts, halves, hidden, acts.reshape(rows, columns)
    )
    grad_back = exchanged(grad_part.reshape(places, capacity, model_width), BACK)
    fwd_part = experts_of(forward_kernel, fwd_rows, parts, halves, hidden)
    fwd_back = exchanged(fwd_part.reshape(places, capacity, model_width), BACK)

    pulled = grad_gates[0] * returned(
        grad_slot, grad_back.reshape(rows, model_width), experts, capacity
    )
    widened = saved_input[0].astype(jnp.float32)
    inverse_rms = lax.rsqrt(jnp.mean(widened * widened, axis=-1, keepdims=True) + epsilon)
    unit_rows = widened * inverse_rms
    weighted = pulled * norm_scale
    through = grads.astype(jnp.float32) + inverse_rms * (
        weighted - unit_rows * jnp.mean(weighted * unit_rows, axis=-1, keepdims=True)
    )
    grad_out = shifted(through.astype(jnp.bfloat16)[None], -1)
    combined = fwd_gates[:, None] * returned(
        fwd_slot, fwd_back.reshape(rows, model_width), experts, capacity
    )
    moved = (tokens.astype(jnp.float32) + combined).astype(jnp.bfloat16)
    return (moved[None], grad_out)


def solution(mesh):
    fine = Mesh(mesh.devices.reshape(4, 4, 2, 4, 4, 2), ("x", "zj", "zp", "y", "zh", "c"))
    expert = ("y", "zh", "c")
    rows = P(PIPE, expert, None)
    placed = (rows,) * 7 + (
        P(PIPE, expert, None, None),
        P(PIPE, None),
        P(expert, None, None),
        P(expert, None, None),
    )
    return jax.shard_map(
        on_device, mesh=fine, in_specs=placed, out_specs=(rows, rows), check_vma=False
    )
```

time: 385 us -> 332 us (0.86)
  waiting for transfers between devices: 183 us -> 109 us
  blocking collectives: 93.2 us -> 110 us
  local copies, waits for them, and re-layouts: 7.72 us -> 15.8 us
  starting transfers between devices: 62 us -> 56.3 us
    all_gather x1, waiting for transfers between devices: 104 us -> 0.02 us  [on_device(): parts = lax.all_gather(part, RING, axis=0)]
    ppermute x0 -> x2, waiting for transfers between devices: none -> 43.7 us  [swapped_rows(): return lax.ppermute(rows, 'zp', [(i, zs - 1 - i) for i in range(zs)])]
    all_to_all x3, blocking collectives: 93.2 us -> 110 us  [exchanged(): return lax.all_to_all(rows, axes, split_axis=0, concat_axis=0, tiled=True)]
    all_to_all x5, waiting for transfers between devices: 62 us -> 55 us  [exchanged(): return lax.all_to_all(rows, axes, split_axis=0, concat_axis=0, tiled=True)]
    ppermute x2 -> x3, starting transfers between devices: 12.6 us -> 6.26 us  [shifted(): lax.ppermute(array, PIPE, [(i, (i + by) % sections) for i in range(sectio...]
    unnamed x26 -> x29, local copies, waits for them, and re-layouts: 5.83 us -> 11.5 us
    ppermute x2 -> x3, waiting for transfers between devices: 16.1 us -> 10.7 us  [shifted(): lax.ppermute(array, PIPE, [(i, (i + by) % sections) for i in range(sectio...]
    pallas_call x1 -> x2, Pallas kernels: 7.78 us -> 7.92 us  [experts_of(): pl.pallas_call(kernel, out_shape=jax.ShapeDtypeStruct((height_rows, width...]
  transfers between devices with their start and end apart: 8 -> 11, of which waited for: 7 -> 8; matrix products, arithmetic and copies ran while one was open for 3% -> 5% of each run, Pallas kernels for 0% -> 2%
where the time goes in v3:
time: 332 us; the launch traced here: 326 us
  blocking collectives  110 us (33%)
  waiting for transfers between devices  109 us (33%)
  starting transfers between devices  56.3 us (17%)
  local copies, waits for them, and re-layouts  15.8 us (5%)
  between operations  14.4 us (4%)
  Pallas kernels  7.92 us (2%)
  other arithmetic  6.35 us (2%)
  matrix products  5.65 us (2%)
    all_to_all x3, blocking collectives, exchanged(): return lax.all_to_all(rows, axes, split_axis=0, concat_axis=0, tiled=True)  110 us
    all_to_all x5, waiting for transfers between devices, exchanged(): return lax.all_to_all(rows, axes, split_axis=0, concat_axis=0, tiled=True)  55 us
    all_to_all x5, starting transfers between devices, exchanged(): return lax.all_to_all(rows, axes, split_axis=0, concat_axis=0, tiled=True)  46.2 us
    ppermute x2, waiting for transfers between devices, swapped_rows(): return lax.ppermute(rows, 'zp', [(i, zs - 1 - i) for i in range(zs)])  43.7 us
    unnamed x29, local copies, waits for them, and re-layouts  11.5 us
    ppermute x3, waiting for transfers between devices, shifted(): lax.ppermute(array, PIPE, [(i, (i + by) % sections) for i in range(sectio...  10.7 us
    pallas_call x2, Pallas kernels, experts_of(): pl.pallas_call(kernel, out_shape=jax.ShapeDtypeStruct((height_rows, width...  7.92 us
  transfers between devices with their start and end apart: 11, of which 8 were waited for; matrix products, arithmetic and copies ran while one was open for 5% of the time, Pallas kernels for 2%

profile of v3, /device:TPU:1, one launch (start us, length us, event | category | flops | bytes accessed | tf_op | source)
XLA Modules:
  0.0 326.1 jit_solution(8650917600874559869)
XLA Ops:
  7.2 1.4 copy-done
  9.6 59.1 %all_to_all.40 = bf16[8,88,128]{2,1,0:T(8,128)(2,1)S(1)} all-to-all(bf16[8,88,128]{2,1,0:T(8,128)(2,1)S(1)} %pad_maximum_fusion), channel_id=1, replica_groups=mesh['x'=4,'zj'=4,'zp'=2,'y'=4,'zh'=4,'c'=2] {'zh','c'}, dimensions={0} | all-to-all | bytes 360448 | tf_op jit(solution)/shard_map/all_to_all | solution.py:64
  68.7 13.1 %all_to_all.41 = bf16[8,88,128]{2,1,0:T(8,128)(2,1)} all-to-all(bf16[8,88,128]{2,1,0:T(8,128)(2,1)S(1)} %all_to_all.40), channel_id=1, replica_groups=mesh['x'=4,'zj'=4,'zp'=2,'y'=4,'zh'=4,'c'=2] {'x','zp'}, dimensions={0} | all-to-all | bytes 360448 | tf_op jit(solution)/shard_map/all_to_all | solution.py:64
  81.9 2.4 collective-permute-start
  86.5 1.9 collective-permute-start.1
  90.4 1.9 collective-permute-start.3
  92.3 10.5 %collective-permute-done.1 = f32[1,3712]{1,0:T(1,128)S(1)} collective-permute-done((f32[1,3712]{1,0:T(1,128)S(1)}, f32[1,3712]{1,0:T(1,128)S(1)}, u32[]{:S(2)}, u32[]{:S(2)}) %collective-permute-start.1) | collective-permute-done | bytes 14880 | tf_op jit(solution)/shard_map/ppermute | solution.py:192
  103.7 1.9 collective-permute-start.2
  106.4 9.0 %all-to-all-start.5 = ((bf16[8,32,512]{2,1,0:T(8,128)(2,1)}), bf16[8,32,512]{2,1,0:T(8,128)(2,1)}, u32[]{:S(2)}, u32[]{:S(2)}) async-start(bf16[8,32,512]{2,1,0:T(8,128)(2,1)} %bitcast.77), calls=%async_computation.5 | async-start | bytes 524288 | tf_op jit(solution)/shard_map/all_to_all | solution.py:64
  115.4 23.0 %collective-permute-done.3 = bf16[64,3584]{1,0:T(8,128)(2,1)} collective-permute-done((bf16[64,3584]{1,0:T(8,128)(2,1)S(1)}, bf16[64,3584]{1,0:T(8,128)(2,1)}, u32[]{:S(2)}, u32[]{:S(2)}) %collective-permute-start.3) | collective-permute-done | bytes 458784 | tf_op jit(solution)/shard_map/ppermute | solution.py:49
  138.4 20.7 %collective-permute-done.2 = bf16[64,3584]{1,0:T(8,128)(2,1)} collective-permute-done((bf16[64,3584]{1,0:T(8,128)(2,1)S(1)}, bf16[64,3584]{1,0:T(8,128)(2,1)}, u32[]{:S(2)}, u32[]{:S(2)}) %collective-permute-start.2) | collective-permute-done | bytes 458784 | tf_op jit(solution)/shard_map/ppermute | solution.py:49
  159.1 2.2 broadcast_select_fusion.1
  161.7 38.0 %all_to_all.42 = bf16[16,16,3584]{2,1,0:T(8,128)(2,1)} all-to-all(bf16[16,16,3584]{2,1,0:T(8,128)(2,1)S(1)} %bitcast.86), channel_id=1, replica_groups=mesh['x'=4,'zj'=4,'zp'=2,'y'=4,'zh'=4,'c'=2] {'x','y'}, dimensions={0} | all-to-all | bytes 3670016 | tf_op jit(solution)/shard_map/all_to_all | solution.py:64
  199.7 20.0 %all-to-all-start.6 = ((bf16[8,32,512]{2,1,0:T(8,128)(2,1)}), bf16[8,32,512]{2,1,0:T(8,128)(2,1)S(1)}, u32[]{:S(2)}, u32[]{:S(2)}) async-start(bf16[8,32,512]{2,1,0:T(8,128)(2,1)} %all-to-all-done.5), calls=%async_computation.6 | async-start | bytes 524288 | tf_op jit(solution)/shard_map/all_to_all | solution.py:64
  219.9 6.0 %all-to-all-done.6 = bf16[8,32,512]{2,1,0:T(8,128)(2,1)S(1)} async-done(((bf16[8,32,512]{2,1,0:T(8,128)(2,1)}), bf16[8,32,512]{2,1,0:T(8,128)(2,1)S(1)}, u32[]{:S(2)}, u32[]{:S(2)}) %all-to-all-start.6) | async-done | bytes 262176 | tf_op jit(solution)/shard_map/all_to_all | solution.py:64
  225.8 1.5 broadcast_in_dim.11
  227.4 4.4 %all-to-all-start = ((bf16[16,16,3584]{2,1,0:T(8,128)(2,1)}), bf16[16,16,3584]{2,1,0:T(8,128)(2,1)}, u32[]{:S(2)}, u32[]{:S(2)}) async-start(bf16[16,16,3584]{2,1,0:T(8,128)(2,1)} %bitcast.85), calls=%async_computation | async-start | bytes 3670016 | tf_op jit(solution)/shard_map/all_to_all | solution.py:64
  231.9 2.6 copy-done.1
  234.5 1.5 copy-done.4
  236.0 4.3 %shard_map.141 = bf16[256,3584]{1,0:T(8,128)(2,1)S(1)} custom-call(bf16[256,3584]{1,0:T(8,128)(2,1)S(1)} %bitcast.82, bf16[32,8,88,128]{3,2,1,0:T(8,128)(2,1)S(1)} %bitcast.79, bf16[256,512]{1,0:T(8,128)(2,1)S(1)} %bitcast.84), custom_call_target="tpu_custom_call" | custom-call | flops 1409286144 | bytes 5767168 | tf_op jit(solution)/shard_map/pallas_call | solution.py:170
  240.3 1.2 copy-done.5
  241.5 11.3 %all-to-all-done = bf16[16,16,3584]{2,1,0:T(8,128)(2,1)} async-done(((bf16[16,16,3584]{2,1,0:T(8,128)(2,1)}), bf16[16,16,3584]{2,1,0:T(8,128)(2,1)}, u32[]{:S(2)}, u32[]{:S(2)}) %all-to-all-start) | async-done | bytes 1835040 | tf_op jit(solution)/shard_map/all_to_all | solution.py:64
  252.8 7.9 %all-to-all-start.7 = ((bf16[32,8,3584]{2,1,0:T(8,128)(2,1)}), bf16[32,8,3584]{2,1,0:T(8,128)(2,1)}, u32[]{:S(2)}, u32[]{:S(2)}) async-start(bf16[32,8,3584]{2,1,0:T(8,128)(2,1)} %bitcast.83), calls=%async_computation.7 | async-start | bytes 3670016 | tf_op jit(solution)/shard_map/all_to_all | solution.py:64
  260.7 2.6 copy-done.2
  263.4 3.7 %shard_map.140 = bf16[256,3584]{1,0:T(8,128)(2,1)S(1)} custom-call(bf16[256,3584]{1,0:T(8,128)(2,1)} %bitcast.10.rows_hbm, bf16[32,8,88,128]{3,2,1,0:T(8,128)(2,1)S(1)} %bitcast.80), custom_call_target="tpu_custom_call" | custom-call | flops 1409286144 | bytes 5767168 | tf_op jit(solution)/shard_map/pallas_call | solution.py:170
  267.0 1.3 copy-done.3
  268.3 17.4 %all-to-all-done.7 = bf16[32,8,3584]{2,1,0:T(8,128)(2,1)} async-done(((bf16[32,8,3584]{2,1,0:T(8,128)(2,1)}), bf16[32,8,3584]{2,1,0:T(8,128)(2,1)}, u32[]{:S(2)}, u32[]{:S(2)}) %all-to-all-start.7) | async-done | bytes 1835040 | tf_op jit(solution)/shard_map/all_to_all | solution.py:64
  285.7 4.9 %all-to-all-start.3 = ((bf16[32,8,3584]{2,1,0:T(8,128)(2,1)}), bf16[32,8,3584]{2,1,0:T(8,128)(2,1)}, u32[]{:S(2)}, u32[]{:S(2)}) async-start(bf16[32,8,3584]{2,1,0:T(8,128)(2,1)} %bitcast.81), calls=%async_computation.3 | async-start | bytes 3670016 | tf_op jit(solution)/shard_map/all_to_all | solution.py:64
  290.8 2.1 fusion.6
  293.3 1.9 collective-permute-start.4
  295.2 20.3 %all-to-all-done.3 = bf16[32,8,3584]{2,1,0:T(8,128)(2,1)} async-done(((bf16[32,8,3584]{2,1,0:T(8,128)(2,1)}), bf16[32,8,3584]{2,1,0:T(8,128)(2,1)}, u32[]{:S(2)}, u32[]{:S(2)}) %all-to-all-start.3) | async-done | bytes 1835040 | tf_op jit(solution)/shard_map/all_to_all | solution.py:64
  315.4 2.8 fusion.16
  (57 shorter events, 8.9 us)
Async XLA Ops:
  7.2 1.5 copy-start
  7.2 82.8 %copy-start.7 = (bf16[1,64,3584]{2,1,0:T(8,128)(2,1)S(1)}, bf16[1,64,3584]{2,1,0:T(8,128)(2,1)}, u32[]{:S(2)}) copy-start(bf16[1,64,3584]{2,1,0:T(8,128)(2,1)} %param.16) | copy-start | bytes 1376260
  7.2 224.7 %all-gather.3.cloned.1.call-start = ((), (), s32[]{:S(2)}) async-start(), calls=%async_computation.8 | async-start | bytes 5947392 | tf_op jit(solution)/shard_map/all_gather | solution.py:224
  9.6 96.0 %copy-start.11 = (bf16[1,1,256,512]{3,2,1,0:T(8,128)(2,1)S(1)}, bf16[1,1,256,512]{3,2,1,0:T(8,128)(2,1)}, u32[]{:S(2)}) copy-start(bf16[1,1,256,512]{3,2,1,0:T(8,128)(2,1)} %param.20) | copy-start | bytes 786436
  81.9 21.2 %collective-permute-start = (bf16[1,64,3584]{2,1,0:T(8,128)(2,1)}, bf16[1,64,3584]{2,1,0:T(8,128)(2,1)S(1)}, u32[]{:S(2)}, u32[]{:S(2)}) collective-permute-start(bf16[1,64,3584]{2,1,0:T(8,128)(2,1)} %param.13), channel_id=1, source_target_pairs={{0,32},{32,64},{64,96},{96,128},{128,160},{160,192},{192,224},{224... | collective-permute-start | bytes 1376264 | tf_op jit(solution)/shard_map/ppermute | solution.py:192
  86.5 16.3 %collective-permute-start.1 = (f32[1,3712]{1,0:T(1,128)S(1)}, f32[1,3712]{1,0:T(1,128)S(1)}, u32[]{:S(2)}, u32[]{:S(2)}) collective-permute-start(f32[1,3712]{1,0:T(1,128)S(1)} %broadcast_in_dim.10), channel_id=1, source_target_pairs={{0,32},{32,64},{64,96},{96,128},{128,160},{160,192},{192,224},{224... | collective-permute-start | bytes 44552 | tf_op jit(solution)/shard_map/ppermute | solution.py:192
  90.4 48.0 %collective-permute-start.3 = (bf16[64,3584]{1,0:T(8,128)(2,1)S(1)}, bf16[64,3584]{1,0:T(8,128)(2,1)}, u32[]{:S(2)}, u32[]{:S(2)}) collective-permute-start(bf16[64,3584]{1,0:T(8,128)(2,1)S(1)} %convolution_convert_fusion), channel_id=1, source_target_pairs={{0,32},{32,0},{1,33},{33,1},{2,34},{34,2},{3,35},{35,3},{4,36},{36... | collective-permute-start | bytes 1376264 | tf_op jit(solution)/shard_map/ppermute | solution.py:49
  103.7 55.4 %collective-permute-start.2 = (bf16[64,3584]{1,0:T(8,128)(2,1)S(1)}, bf16[64,3584]{1,0:T(8,128)(2,1)}, u32[]{:S(2)}, u32[]{:S(2)}) collective-permute-start(bf16[64,3584]{1,0:T(8,128)(2,1)S(1)} %convolution_convert_fusion.1), channel_id=1, source_target_pairs={{0,32},{32,0},{1,33},{33,1},{2,34},{34,2},{3,35},{35,3},{4,36},{36... | collective-permute-start | bytes 1376264 | tf_op jit(solution)/shard_map/ppermute | solution.py:49
  106.4 55.1 %all-to-all-start.5 = ((bf16[8,32,512]{2,1,0:T(8,128)(2,1)}), bf16[8,32,512]{2,1,0:T(8,128)(2,1)}, u32[]{:S(2)}, u32[]{:S(2)}) async-start(bf16[8,32,512]{2,1,0:T(8,128)(2,1)} %bitcast.77), calls=%async_computation.5 | async-start | bytes 524288 | tf_op jit(solution)/shard_map/all_to_all | solution.py:64
  161.7 58.0 %copy-start.9 = (bf16[64,3584]{1,0:T(8,128)(2,1)S(1)}, bf16[64,3584]{1,0:T(8,128)(2,1)}, u32[]{:S(2)}) copy-start(bf16[64,3584]{1,0:T(8,128)(2,1)} %get-tuple-element.10) | copy-start | bytes 1376260
  161.7 58.0 %copy-start.10 = (bf16[64,3584]{1,0:T(8,128)(2,1)S(1)}, bf16[64,3584]{1,0:T(8,128)(2,1)}, u32[]{:S(2)}) copy-start(bf16[64,3584]{1,0:T(8,128)(2,1)} %get-tuple-element.11) | copy-start | bytes 1376260
  199.7 26.1 %all-to-all-start.6 = ((bf16[8,32,512]{2,1,0:T(8,128)(2,1)}), bf16[8,32,512]{2,1,0:T(8,128)(2,1)S(1)}, u32[]{:S(2)}, u32[]{:S(2)}) async-start(bf16[8,32,512]{2,1,0:T(8,128)(2,1)} %all-to-all-done.5), calls=%async_computation.6 | async-start | bytes 524288 | tf_op jit(solution)/shard_map/all_to_all | solution.py:64
  227.4 25.5 %all-to-all-start = ((bf16[16,16,3584]{2,1,0:T(8,128)(2,1)}), bf16[16,16,3584]{2,1,0:T(8,128)(2,1)}, u32[]{:S(2)}, u32[]{:S(2)}) async-start(bf16[16,16,3584]{2,1,0:T(8,128)(2,1)} %bitcast.85), calls=%async_computation | async-start | bytes 3670016 | tf_op jit(solution)/shard_map/all_to_all | solution.py:64
  231.9 2.6 copy-start.1
  234.5 1.5 copy-start.4
  240.3 1.2 copy-start.5
  252.8 32.9 %all-to-all-start.7 = ((bf16[32,8,3584]{2,1,0:T(8,128)(2,1)}), bf16[32,8,3584]{2,1,0:T(8,128)(2,1)}, u32[]{:S(2)}, u32[]{:S(2)}) async-start(bf16[32,8,3584]{2,1,0:T(8,128)(2,1)} %bitcast.83), calls=%async_computation.7 | async-start | bytes 3670016 | tf_op jit(solution)/shard_map/all_to_all | solution.py:64
  260.7 2.6 copy-start.2
  267.0 1.3 copy-start.3
  285.7 4.9 %copy-start.6 = (bf16[1,64,3584]{2,1,0:T(8,128)(2,1)S(1)}, bf16[1,64,3584]{2,1,0:T(8,128)(2,1)}, u32[]{:S(2)}) copy-start(bf16[1,64,3584]{2,1,0:T(8,128)(2,1)} %param.19) | copy-start | bytes 1376260
  285.7 5.1 %copy-start.12 = (s32[256]{0:T(256)S(1)}, s32[256]{0:T(256)}, u32[]{:S(2)}) copy-start(s32[256]{0:T(256)} %constant.55) | copy-start | bytes 3076
  285.7 5.1 %copy-start.13 = (f32[1,64,1]{1,2,0:T(1,128)S(1)}, f32[1,64,1]{1,2,0:T(1,128)}, u32[]{:S(2)}) copy-start(f32[1,64,1]{1,2,0:T(1,128)} %param.18) | copy-start | bytes 772
  285.7 29.7 %all-to-all-start.3 = ((bf16[32,8,3584]{2,1,0:T(8,128)(2,1)}), bf16[32,8,3584]{2,1,0:T(8,128)(2,1)}, u32[]{:S(2)}, u32[]{:S(2)}) async-start(bf16[32,8,3584]{2,1,0:T(8,128)(2,1)} %bitcast.81), calls=%async_computation.3 | async-start | bytes 3670016 | tf_op jit(solution)/shard_map/all_to_all | solution.py:64
  290.6 2.3 copy-start.8
  293.3 25.2 %collective-permute-start.4 = (bf16[1,64,3584]{2,1,0:T(8,128)(2,1)S(1)}, bf16[1,64,3584]{2,1,0:T(8,128)(2,1)S(1)}, u32[]{:S(2)}, u32[]{:S(2)}) collective-permute-start(bf16[1,64,3584]{2,1,0:T(8,128)(2,1)S(1)} %fusion.18), channel_id=1, source_target_pairs={{0,992},{32,0},{64,32},{96,64},{128,96},{160,128},{192,160},{224,1... | collective-permute-start | bytes 1376264 | tf_op jit(solution)/shard_map/ppermute | solution.py:192
Sparse Core Ops, SparseCore 0:
  82.0 126.5 all-gather.2

commit v4 on v3

--- a/solution.py
+++ b/solution.py
@@ -114,9 +114,24 @@
     return first_copies, second_copies
 
 
-def forward_kernel(rows_hbm, parts_ref, out_ref, rows_ref, first_ref, second_ref, sems):
+def written(strip, out_hbm, out_ref, done):
+    width = out_ref.shape[1] // done.shape[0]
+    copies = []
+    for q in range(done.shape[0]):
+        part = slice(q * width, (q + 1) * width)
+        out_ref[:, part] = strip(part).astype(jnp.bfloat16)
+        columns_of = pl.ds(q * width, width)
+        copies.append(
+            pltpu.make_async_copy(out_ref.at[:, columns_of], out_hbm.at[:, columns_of], done.at[q])
+        )
+        copies[-1].start()
+    for copy in copies:
+        copy.wait()
+
+
+def forward_kernel(rows_hbm, parts_ref, out_hbm, rows_ref, out_ref, first_ref, second_ref, sems, done):
     parts, halves, tall, columns = first_ref.shape
-    _, deep, width = second_ref.shape
+    _, deep, _ = second_ref.shape
     hidden = parts * deep
     first_copies, second_copies = weight_copies(parts_ref, first_ref, second_ref, sems)
     rows_copy = pltpu.make_async_copy(rows_hbm, rows_ref, sems.at[0])
@@ -130,12 +145,18 @@
     mixed = (gate / (1.0 + jnp.exp(-gate)) * up).astype(jnp.bfloat16)
     for copy in second_copies:
         copy.wait()
-    second = second_ref[...].reshape(hidden, width)
-    out_ref[...] = jnp.dot(mixed, second, preferred_element_type=jnp.float32).astype(jnp.bfloat16)
-
-
-def gradient_kernel(rows_hbm, parts_ref, acts_ref, out_ref, rows_ref, first_ref, second_ref, sems):
-    parts, halves, tall, columns = first_ref.shape
+
+    def strip(columns_of):
+        second = second_ref[:, :, columns_of].reshape(hidden, -1)
+        return jnp.dot(mixed, second, preferred_element_type=jnp.float32)
+
+    written(strip, out_hbm, out_ref, done)
+
+
+def gradient_kernel(
+    rows_hbm, parts_ref, acts_ref, out_hbm, rows_ref, out_ref, first_ref, second_ref, sems, done
+):
+    parts, _, _, columns = first_ref.shape
     _, deep, width = second_ref.shape
     hidden = parts * deep
     first_copies, second_copies = weight_copies(parts_ref, first_ref, second_ref, sems)
@@ -155,10 +176,15 @@
     joined = jnp.concatenate([gate_grad.astype(jnp.bfloat16), up_grad.astype(jnp.bfloat16)], axis=1)
     for copy in first_copies:
         copy.wait()
-    first = first_ref[...].reshape(parts * halves * tall, columns)
-    out_ref[...] = lax.dot_general(
-        joined, first, turned, preferred_element_type=jnp.float32
-    ).astype(jnp.bfloat16)
+
+    first = first_ref[...].reshape(width, columns)
+
+    def strip(columns_of):
+        return lax.dot_general(
+            joined, first[columns_of, :], turned, preferred_element_type=jnp.float32
+        )
+
+    written(strip, out_hbm, out_ref, done)
 
 
 def experts_of(kernel, rows, parts, halves, hidden, *more):
@@ -166,17 +192,19 @@
     height_rows, width = rows.shape
     columns = 2 * hidden
     deep, tall = hidden // count, width // count // halves
-    vmem, hbm = pl.BlockSpec(memory_space=pltpu.VMEM), pl.BlockSpec(memory_space=pl.ANY)
+    vmem, hbm = pl.BlockSpec(memory_space=pltpu.VMEM), pl.BlockSpec(memory_space=pltpu.HBM)
     return pl.pallas_call(
         kernel,
-        out_shape=jax.ShapeDtypeStruct((height_rows, width), jnp.bfloat16),
+        out_shape=pltpu.HBM((height_rows, width), jnp.bfloat16),
         in_specs=[hbm, hbm] + [vmem] * len(more),
-        out_specs=vmem,
+        out_specs=hbm,
         scratch_shapes=[
+            pltpu.VMEM((height_rows, width), jnp.bfloat16),
             pltpu.VMEM((height_rows, width), jnp.bfloat16),
             pltpu.VMEM((count, halves, tall, columns), jnp.bfloat16),
             pltpu.VMEM((count, deep, width), jnp.bfloat16),
             pltpu.SemaphoreType.DMA((1 + pieces + width // wide,)),
+            pltpu.SemaphoreType.DMA((width // columns,)),
         ],
         compiler_params=pltpu.CompilerParams(vmem_limit_bytes=32 * 1024 * 1024),
         cost_estimate=pl.CostEstimate(
@@ -184,7 +212,7 @@
             bytes_accessed=count * pieces * height * wide * 2,
             transcendentals=height_rows * hidden,
         ),
-    )(rows, parts, *more)
+    )(pltpu.with_memory_space_constraint(rows, pltpu.HBM), pltpu.with_memory_space_constraint(parts, pltpu.HBM), *more)
 
 
 def shifted(array, by):
@@ -227,16 +255,9 @@
     grad_own = grouped(grad_slot, grads)
     grad_partner = swapped_rows(grad_own)
 
-    small = jnp.concatenate(
-        [norm_scale, forward_ids[0, :, 0].astype(jnp.float32), forward_gates[0, :, 0]]
-    )
-    tokens = shifted(forward_in, 1)[0]
-    small = shifted(small[None], 1)[0]
-    fwd_scale = small[:model_width]
-    fwd_ids = small[model_width : model_width + token_count].astype(jnp.int32)
-    fwd_gates = small[model_width + token_count :]
-    fwd_slot = slots(fwd_ids[:, None], capacity)
-    fwd_own = grouped(fwd_slot, normalize(tokens, fwd_scale))
+    tokens = forward_in[0]
+    fwd_slot = slots(forward_ids[0], capacity)
+    fwd_own = grouped(fwd_slot, normalize(tokens, norm_scale))
     fwd_partner = swapped_rows(fwd_own)
 
     xs, zs, ys, far = lax.axis_size("x"), lax.axis_size("zp"), lax.axis_size("y"), lax.axis_size(FAR)
@@ -268,11 +289,12 @@
         weighted - unit_rows * jnp.mean(weighted * unit_rows, axis=-1, keepdims=True)
     )
     grad_out = shifted(through.astype(jnp.bfloat16)[None], -1)
-    combined = fwd_gates[:, None] * returned(
+    combined = forward_gates[0] * returned(
         fwd_slot, fwd_back.reshape(rows, model_width), experts, capacity
     )
     moved = (tokens.astype(jnp.float32) + combined).astype(jnp.bfloat16)
-    return (moved[None], grad_out)
+    forward_out = shifted(moved[None], 1)
+    return (forward_out, grad_out)
 
 
 def solution(mesh):

time: 332 us -> 316 us (0.952)
  the two profiles are of different devices: /device:TPU:1 before, /device:TPU:16 now
where the time goes in v4:
time: 316 us; the launch traced here: 315 us
  waiting for transfers between devices  124 us (39%)
  starting transfers between devices  75.6 us (24%)
  blocking collectives  72.9 us (23%)
  between operations  14.3 us (5%)
  Pallas kernels  11.5 us (4%)
  local copies, waits for them, and re-layouts  8.75 us (3%)
  matrix products  4.88 us (2%)
    all_to_all x2, blocking collectives, exchanged(): return lax.all_to_all(rows, axes, split_axis=0, concat_axis=0, tiled=True)  72.9 us
    all_to_all x6, waiting for transfers between devices, exchanged(): return lax.all_to_all(rows, axes, split_axis=0, concat_axis=0, tiled=True)  65.8 us
    all_to_all x6, starting transfers between devices, exchanged(): return lax.all_to_all(rows, axes, split_axis=0, concat_axis=0, tiled=True)  47.1 us
    ppermute x2, waiting for transfers between devices, swapped_rows(): return lax.ppermute(rows, 'zp', [(i, zs - 1 - i) for i in range(zs)])  28 us
    ppermute x2, waiting for transfers between devices, shifted(): lax.ppermute(array, PIPE, [(i, (i + by) % sections) for i in range(sectio...  20.4 us
    ppermute x2, starting transfers between devices, shifted(): lax.ppermute(array, PIPE, [(i, (i + by) % sections) for i in range(sectio...  15.6 us
    ppermute x2, starting transfers between devices, swapped_rows(): return lax.ppermute(rows, 'zp', [(i, zs - 1 - i) for i in range(zs)])  12.9 us
    pallas_call x2, Pallas kernels, experts_of(): pl.pallas_call(kernel, out_shape=pltpu.HBM((height_rows, width), jnp.bflo...  11.5 us
  transfers between devices with their start and end apart: 11, of which 10 were waited for; matrix products, arithmetic and copies ran while one was open for 4% of the time, Pallas kernels for 4%

profile of v4, /device:TPU:16, one launch (start us, length us, event | category | flops | bytes accessed | tf_op | source)
XLA Modules:
  0.0 314.6 jit_solution(7059630281266081116)
XLA Ops:
  7.3 1.4 copy-done
  8.7 0.9 constant_dynamic-slice_fusion.1
  9.6 58.4 %all_to_all.40 = bf16[8,88,128]{2,1,0:T(8,128)(2,1)S(1)} all-to-all(bf16[8,88,128]{2,1,0:T(8,128)(2,1)S(1)} %pad_maximum_fusion), channel_id=1, replica_groups=mesh['x'=4,'zj'=4,'zp'=2,'y'=4,'zh'=4,'c'=2] {'zh','c'}, dimensions={0} | all-to-all | bytes 360448 | tf_op jit(solution)/shard_map/all_to_all | solution.py:64
  68.0 14.5 %all_to_all.41 = bf16[8,88,128]{2,1,0:T(8,128)(2,1)} all-to-all(bf16[8,88,128]{2,1,0:T(8,128)(2,1)S(1)} %all_to_all.40), channel_id=1, replica_groups=mesh['x'=4,'zj'=4,'zp'=2,'y'=4,'zh'=4,'c'=2] {'x','zp'}, dimensions={0} | all-to-all | bytes 360448 | tf_op jit(solution)/shard_map/all_to_all | solution.py:64
  82.6 0.9 convert_reduce_fusion
  84.6 2.7 collective-permute-start.2
  88.0 5.1 %all-to-all-start.5 = ((bf16[8,32,512]{2,1,0:T(8,128)(2,1)}), bf16[8,32,512]{2,1,0:T(8,128)(2,1)}, u32[]{:S(2)}, u32[]{:S(2)}) async-start(bf16[8,32,512]{2,1,0:T(8,128)(2,1)} %bitcast.69), calls=%async_computation.5 | async-start | bytes 524288 | tf_op jit(solution)/shard_map/all_to_all | solution.py:64
  93.2 28.0 %collective-permute-done.2 = bf16[64,3584]{1,0:T(8,128)(2,1)S(1)} collective-permute-done((bf16[64,3584]{1,0:T(8,128)(2,1)S(1)}, bf16[64,3584]{1,0:T(8,128)(2,1)S(1)}, u32[]{:S(2)}, u32[]{:S(2)}) %collective-permute-start.2) | collective-permute-done | bytes 458784 | tf_op jit(solution)/shard_map/ppermute | solution.py:49
  121.4 14.9 %all-to-all-done.5 = bf16[8,32,512]{2,1,0:T(8,128)(2,1)} async-done(((bf16[8,32,512]{2,1,0:T(8,128)(2,1)}), bf16[8,32,512]{2,1,0:T(8,128)(2,1)}, u32[]{:S(2)}, u32[]{:S(2)}) %all-to-all-start.5) | async-done | bytes 262176 | tf_op jit(solution)/shard_map/all_to_all | solution.py:64
  136.2 1.5 broadcast_in_dim.10
  137.7 5.0 %all-to-all-start.4 = ((bf16[16,16,3584]{2,1,0:T(8,128)(2,1)}), bf16[16,16,3584]{2,1,0:T(8,128)(2,1)}, u32[]{:S(2)}, u32[]{:S(2)}) async-start(bf16[16,16,3584]{2,1,0:T(8,128)(2,1)} %bitcast.76), calls=%async_computation.4 | async-start | bytes 3670016 | tf_op jit(solution)/shard_map/all_to_all | solution.py:64
  143.5 10.2 %collective-permute-start = (bf16[64,3584]{1,0:T(8,128)(2,1)S(1)}, bf16[64,3584]{1,0:T(8,128)(2,1)S(1)}, u32[]{:S(2)}, u32[]{:S(2)}) collective-permute-start(bf16[64,3584]{1,0:T(8,128)(2,1)S(1)} %convolution_convert_fusion.1), channel_id=1, source_target_pairs={{0,32},{32,0},{1,33},{33,1},{2,34},{34,2},{3,35},{35,3},{4,36},{36... | collective-permute-start | bytes 1376264 | tf_op jit(solution)/shard_map/ppermute | solution.py:49
  153.7 11.9 %all-to-all-done.4 = bf16[16,16,3584]{2,1,0:T(8,128)(2,1)} async-done(((bf16[16,16,3584]{2,1,0:T(8,128)(2,1)}), bf16[16,16,3584]{2,1,0:T(8,128)(2,1)}, u32[]{:S(2)}, u32[]{:S(2)}) %all-to-all-start.4) | async-done | bytes 1835040 | tf_op jit(solution)/shard_map/all_to_all | solution.py:64
  165.6 12.3 %all-to-all-start.6 = ((bf16[8,32,512]{2,1,0:T(8,128)(2,1)}), bf16[8,32,512]{2,1,0:T(8,128)(2,1)S(1)}, u32[]{:S(2)}, u32[]{:S(2)}) async-start(bf16[8,32,512]{2,1,0:T(8,128)(2,1)} %all-to-all-done.5), calls=%async_computation.6 | async-start | bytes 524288 | tf_op jit(solution)/shard_map/all_to_all | solution.py:64
  178.1 9.1 %all-to-all-done.6 = bf16[8,32,512]{2,1,0:T(8,128)(2,1)S(1)} async-done(((bf16[8,32,512]{2,1,0:T(8,128)(2,1)}), bf16[8,32,512]{2,1,0:T(8,128)(2,1)S(1)}, u32[]{:S(2)}, u32[]{:S(2)}) %all-to-all-start.6) | async-done | bytes 262176 | tf_op jit(solution)/shard_map/all_to_all | solution.py:64
  187.2 1.5 broadcast_in_dim.8
  188.8 6.9 %all-to-all-start = ((bf16[16,16,3584]{2,1,0:T(8,128)(2,1)}), bf16[16,16,3584]{2,1,0:T(8,128)(2,1)}, u32[]{:S(2)}, u32[]{:S(2)}) async-start(bf16[16,16,3584]{2,1,0:T(8,128)(2,1)} %bitcast.77), calls=%async_computation | async-start | bytes 3670016 | tf_op jit(solution)/shard_map/all_to_all | solution.py:64
  195.6 1.0 copy.33
  196.6 9.7 %all-gather.3.cloned.1.call-done = bf16[256,88,128]{2,1,0:T(8,128)(2,1)} async-done(((bf16[8,88,128]{2,1,0:T(8,128)(2,1)}), bf16[256,88,128]{2,1,0:T(8,128)(2,1)}) %all-gather.3.cloned.1.call-update) | async-done | bytes 5767184 | tf_op jit(solution)/shard_map/all_gather | solution.py:252
  206.3 5.8 %shard_map.141 = bf16[256,3584]{1,0:T(8,128)(2,1)} custom-call(bf16[256,3584]{1,0:T(8,128)(2,1)} %bitcast.27.rows_hbm, bf16[32,8,88,128]{3,2,1,0:T(8,128)(2,1)} %bitcast.72, bf16[256,512]{1,0:T(8,128)(2,1)S(1)} %bitcast.71), custom_call_target="tpu_custom_call" | custom-call | flops 1409286144 | bytes 5767168 | tf_op jit(solution)/shard_map/pallas_call | solution.py:196
  212.1 6.1 %all-to-all-done = bf16[16,16,3584]{2,1,0:T(8,128)(2,1)} async-done(((bf16[16,16,3584]{2,1,0:T(8,128)(2,1)}), bf16[16,16,3584]{2,1,0:T(8,128)(2,1)}, u32[]{:S(2)}, u32[]{:S(2)}) %all-to-all-start) | async-done | bytes 1835040 | tf_op jit(solution)/shard_map/all_to_all | solution.py:64
  218.2 8.8 %all-to-all-start.7 = ((bf16[32,8,3584]{2,1,0:T(8,128)(2,1)}), bf16[32,8,3584]{2,1,0:T(8,128)(2,1)}, u32[]{:S(2)}, u32[]{:S(2)}) async-start(bf16[32,8,3584]{2,1,0:T(8,128)(2,1)} %bitcast.75), calls=%async_computation.7 | async-start | bytes 3670016 | tf_op jit(solution)/shard_map/all_to_all | solution.py:64
  227.0 5.7 %shard_map.140 = bf16[256,3584]{1,0:T(8,128)(2,1)} custom-call(bf16[256,3584]{1,0:T(8,128)(2,1)} %bitcast.8.rows_hbm, bf16[32,8,88,128]{3,2,1,0:T(8,128)(2,1)} %bitcast.73), custom_call_target="tpu_custom_call" | custom-call | flops 1409286144 | bytes 5767168 | tf_op jit(solution)/shard_map/pallas_call | solution.py:196
  232.7 15.5 %all-to-all-done.7 = bf16[32,8,3584]{2,1,0:T(8,128)(2,1)} async-done(((bf16[32,8,3584]{2,1,0:T(8,128)(2,1)}), bf16[32,8,3584]{2,1,0:T(8,128)(2,1)}, u32[]{:S(2)}, u32[]{:S(2)}) %all-to-all-start.7) | async-done | bytes 1835040 | tf_op jit(solution)/shard_map/all_to_all | solution.py:64
  248.2 9.0 %all-to-all-start.3 = ((bf16[32,8,3584]{2,1,0:T(8,128)(2,1)}), bf16[32,8,3584]{2,1,0:T(8,128)(2,1)}, u32[]{:S(2)}, u32[]{:S(2)}) async-start(bf16[32,8,3584]{2,1,0:T(8,128)(2,1)} %bitcast.74), calls=%async_computation.3 | async-start | bytes 3670016 | tf_op jit(solution)/shard_map/all_to_all | solution.py:64
  257.5 2.1 fusion.8
  259.9 12.6 %collective-permute-start.3 = (bf16[1,64,3584]{2,1,0:T(8,128)(2,1)S(1)}, bf16[1,64,3584]{2,1,0:T(8,128)(2,1)S(1)}, u32[]{:S(2)}, u32[]{:S(2)}) collective-permute-start(bf16[1,64,3584]{2,1,0:T(8,128)(2,1)S(1)} %fusion.18), channel_id=1, source_target_pairs={{0,992},{32,0},{64,32},{96,64},{128,96},{160,128},{192,160},{224,1... | collective-permute-start | bytes 1376264 | tf_op jit(solution)/shard_map/ppermute | solution.py:220
  272.6 8.3 %all-to-all-done.3 = bf16[32,8,3584]{2,1,0:T(8,128)(2,1)} async-done(((bf16[32,8,3584]{2,1,0:T(8,128)(2,1)}), bf16[32,8,3584]{2,1,0:T(8,128)(2,1)}, u32[]{:S(2)}, u32[]{:S(2)}) %all-to-all-start.3) | async-done | bytes 1835040 | tf_op jit(solution)/shard_map/all_to_all | solution.py:64
  280.9 2.0 fusion.3
  282.8 3.0 collective-permute-start.1
  285.8 2.3 collective-permute-done.3
  288.2 18.1 %collective-permute-done.1 = bf16[1,64,3584]{2,1,0:T(8,128)(2,1)S(1)} collective-permute-done((bf16[1,64,3584]{2,1,0:T(8,128)(2,1)S(1)}, bf16[1,64,3584]{2,1,0:T(8,128)(2,1)S(1)}, u32[]{:S(2)}, u32[]{:S(2)}) %collective-permute-start.1) | collective-permute-done | bytes 458784 | tf_op jit(solution)/shard_map/ppermute | solution.py:220
  (49 shorter events, 5.2 us)
Async XLA Ops:
  7.2 1.5 copy-start
  7.2 77.0 %copy-start.3 = (bf16[1,64,3584]{2,1,0:T(8,128)(2,1)S(1)}, bf16[1,64,3584]{2,1,0:T(8,128)(2,1)}, u32[]{:S(2)}) copy-start(bf16[1,64,3584]{2,1,0:T(8,128)(2,1)} %param.16) | copy-start | bytes 1376260
  7.2 80.1 %copy-start.6 = (bf16[1,1,256,512]{3,2,1,0:T(8,128)(2,1)S(1)}, bf16[1,1,256,512]{3,2,1,0:T(8,128)(2,1)}, u32[]{:S(2)}) copy-start(bf16[1,1,256,512]{3,2,1,0:T(8,128)(2,1)} %param.20) | copy-start | bytes 786436
  7.2 199.1 %all-gather.3.cloned.1.call-start = ((), (), s32[]{:S(2)}) async-start(), calls=%async_computation.8 | async-start | bytes 5947392 | tf_op jit(solution)/shard_map/all_gather | solution.py:252
  84.6 36.6 %collective-permute-start.2 = (bf16[64,3584]{1,0:T(8,128)(2,1)S(1)}, bf16[64,3584]{1,0:T(8,128)(2,1)S(1)}, u32[]{:S(2)}, u32[]{:S(2)}) collective-permute-start(bf16[64,3584]{1,0:T(8,128)(2,1)S(1)} %convolution_convert_fusion), channel_id=1, source_target_pairs={{0,32},{32,0},{1,33},{33,1},{2,34},{34,2},{3,35},{35,3},{4,36},{36... | collective-permute-start | bytes 1376264 | tf_op jit(solution)/shard_map/ppermute | solution.py:49
  88.0 48.2 %all-to-all-start.5 = ((bf16[8,32,512]{2,1,0:T(8,128)(2,1)}), bf16[8,32,512]{2,1,0:T(8,128)(2,1)}, u32[]{:S(2)}, u32[]{:S(2)}) async-start(bf16[8,32,512]{2,1,0:T(8,128)(2,1)} %bitcast.69), calls=%async_computation.5 | async-start | bytes 524288 | tf_op jit(solution)/shard_map/all_to_all | solution.py:64
  137.7 5.0 %copy-start.7 = (f32[1,3584]{1,0:T(1,128)S(1)}, f32[1,3584]{1,0:T(1,128)}, u32[]{:S(2)}) copy-start(f32[1,3584]{1,0:T(1,128)} %param.21) | copy-start | bytes 43012
  137.7 5.0 %copy-start.11 = (s32[1,64,1]{1,2,0:T(1,128)S(1)}, s32[1,64,1]{1,2,0:T(1,128)}, u32[]{:S(2)}) copy-start(s32[1,64,1]{1,2,0:T(1,128)} %param.14) | copy-start | bytes 772
  137.7 5.2 %copy-start.1 = (bf16[1,64,3584]{2,1,0:T(8,128)(2,1)S(1)}, bf16[1,64,3584]{2,1,0:T(8,128)(2,1)}, u32[]{:S(2)}) copy-start(bf16[1,64,3584]{2,1,0:T(8,128)(2,1)} %param.13) | copy-start | bytes 1376260
  137.7 27.9 %all-to-all-start.4 = ((bf16[16,16,3584]{2,1,0:T(8,128)(2,1)}), bf16[16,16,3584]{2,1,0:T(8,128)(2,1)}, u32[]{:S(2)}, u32[]{:S(2)}) async-start(bf16[16,16,3584]{2,1,0:T(8,128)(2,1)} %bitcast.76), calls=%async_computation.4 | async-start | bytes 3670016 | tf_op jit(solution)/shard_map/all_to_all | solution.py:64
  143.5 34.4 %collective-permute-start = (bf16[64,3584]{1,0:T(8,128)(2,1)S(1)}, bf16[64,3584]{1,0:T(8,128)(2,1)S(1)}, u32[]{:S(2)}, u32[]{:S(2)}) collective-permute-start(bf16[64,3584]{1,0:T(8,128)(2,1)S(1)} %convolution_convert_fusion.1), channel_id=1, source_target_pairs={{0,32},{32,0},{1,33},{33,1},{2,34},{34,2},{3,35},{35,3},{4,36},{36... | collective-permute-start | bytes 1376264 | tf_op jit(solution)/shard_map/ppermute | solution.py:49
  165.6 21.7 %all-to-all-start.6 = ((bf16[8,32,512]{2,1,0:T(8,128)(2,1)}), bf16[8,32,512]{2,1,0:T(8,128)(2,1)S(1)}, u32[]{:S(2)}, u32[]{:S(2)}) async-start(bf16[8,32,512]{2,1,0:T(8,128)(2,1)} %all-to-all-done.5), calls=%async_computation.6 | async-start | bytes 524288 | tf_op jit(solution)/shard_map/all_to_all | solution.py:64
  187.2 1.5 copy-start.5
  188.8 29.5 %all-to-all-start = ((bf16[16,16,3584]{2,1,0:T(8,128)(2,1)}), bf16[16,16,3584]{2,1,0:T(8,128)(2,1)}, u32[]{:S(2)}, u32[]{:S(2)}) async-start(bf16[16,16,3584]{2,1,0:T(8,128)(2,1)} %bitcast.77), calls=%async_computation | async-start | bytes 3670016 | tf_op jit(solution)/shard_map/all_to_all | solution.py:64
  218.2 30.0 %all-to-all-start.7 = ((bf16[32,8,3584]{2,1,0:T(8,128)(2,1)}), bf16[32,8,3584]{2,1,0:T(8,128)(2,1)}, u32[]{:S(2)}, u32[]{:S(2)}) async-start(bf16[32,8,3584]{2,1,0:T(8,128)(2,1)} %bitcast.75), calls=%async_computation.7 | async-start | bytes 3670016 | tf_op jit(solution)/shard_map/all_to_all | solution.py:64
  248.2 9.0 %copy-start.2 = (bf16[1,64,3584]{2,1,0:T(8,128)(2,1)S(1)}, bf16[1,64,3584]{2,1,0:T(8,128)(2,1)}, u32[]{:S(2)}) copy-start(bf16[1,64,3584]{2,1,0:T(8,128)(2,1)} %param.19) | copy-start | bytes 1376260
  248.2 9.3 %copy-start.8 = (s32[256]{0:T(256)S(1)}, s32[256]{0:T(256)}, u32[]{:S(2)}) copy-start(s32[256]{0:T(256)} %constant.55) | copy-start | bytes 3076
  248.2 9.3 %copy-start.10 = (f32[1,64,1]{1,2,0:T(1,128)S(1)}, f32[1,64,1]{1,2,0:T(1,128)}, u32[]{:S(2)}) copy-start(f32[1,64,1]{1,2,0:T(1,128)} %param.18) | copy-start | bytes 772
  248.2 32.6 %all-to-all-start.3 = ((bf16[32,8,3584]{2,1,0:T(8,128)(2,1)}), bf16[32,8,3584]{2,1,0:T(8,128)(2,1)}, u32[]{:S(2)}, u32[]{:S(2)}) async-start(bf16[32,8,3584]{2,1,0:T(8,128)(2,1)} %bitcast.74), calls=%async_computation.3 | async-start | bytes 3670016 | tf_op jit(solution)/shard_map/all_to_all | solution.py:64
  257.3 2.4 copy-start.4
  259.6 21.2 %copy-start.9 = (f32[1,64,1]{1,2,0:T(1,128)S(1)}, f32[1,64,1]{1,2,0:T(1,128)}, u32[]{:S(2)}) copy-start(f32[1,64,1]{1,2,0:T(1,128)} %param.15) | copy-start | bytes 772
  259.9 28.2 %collective-permute-start.3 = (bf16[1,64,3584]{2,1,0:T(8,128)(2,1)S(1)}, bf16[1,64,3584]{2,1,0:T(8,128)(2,1)S(1)}, u32[]{:S(2)}, u32[]{:S(2)}) collective-permute-start(bf16[1,64,3584]{2,1,0:T(8,128)(2,1)S(1)} %fusion.18), channel_id=1, source_target_pairs={{0,992},{32,0},{64,32},{96,64},{128,96},{160,128},{192,160},{224,1... | collective-permute-start | bytes 1376264 | tf_op jit(solution)/shard_map/ppermute | solution.py:220
  282.8 23.4 %collective-permute-start.1 = (bf16[1,64,3584]{2,1,0:T(8,128)(2,1)S(1)}, bf16[1,64,3584]{2,1,0:T(8,128)(2,1)S(1)}, u32[]{:S(2)}, u32[]{:S(2)}) collective-permute-start(bf16[1,64,3584]{2,1,0:T(8,128)(2,1)S(1)} %fusion.3), channel_id=1, source_target_pairs={{0,32},{32,64},{64,96},{96,128},{128,160},{160,192},{192,224},{224... | collective-permute-start | bytes 1376264 | tf_op jit(solution)/shard_map/ppermute | solution.py:220
Sparse Core Ops, SparseCore 0:
  82.7 123.5 all-gather.2

commit v5 on v4

--- a/solution.py
+++ b/solution.py
@@ -215,6 +215,37 @@
     )(pltpu.with_memory_space_constraint(rows, pltpu.HBM), pltpu.with_memory_space_constraint(parts, pltpu.HBM), *more)
 
 
+def moved_acts(acts):
+    axes = ("x", "zp", "zh", "c")
+    xs, zs, blocks, cs = (lax.axis_size(axis) for axis in axes)
+    x, zp, zh, c = (lax.axis_index(axis) for axis in axes)
+
+    def flat(a, b, k, m):
+        return ((a * zs + b) * blocks + k) * cs + m
+
+    got = []
+    for dk in range(blocks):
+        for dm in range(cs):
+            pairs = [
+                (flat(i, j, k, m), flat(k, m, (i + dk) % blocks, (j + dm) % cs))
+                for i, j, k, m in np.ndindex(xs, zs, blocks, cs)
+            ]
+            piece = lax.dynamic_index_in_dim(
+                acts, (x + dk) % blocks * cs + (zp + dm) % cs, 0, keepdims=False
+            )
+            got.append(lax.ppermute(piece, axes, pairs))
+    got = jnp.stack(got)
+    return jnp.stack(
+        [
+            lax.dynamic_index_in_dim(
+                got, (zh - i) % blocks * cs + (c - j) % cs, 0, keepdims=False
+            )
+            for i in range(xs)
+            for j in range(zs)
+        ]
+    )
+
+
 def shifted(array, by):
     sections = lax.axis_size(PIPE)
     return lax.ppermute(array, PIPE, [(i, (i + by) % sections) for i in range(sections)])
@@ -262,8 +293,7 @@
 
     xs, zs, ys, far = lax.axis_size("x"), lax.axis_size("zp"), lax.axis_size("y"), lax.axis_size(FAR)
     acts = saved_acts[0, 0].reshape(ys, far, capacity, columns).transpose(1, 0, 2, 3)
-    acts = exchanged(acts.reshape(far, ys * capacity, columns), FAR)
-    acts = exchanged(acts, NEAR)
+    acts = moved_acts(acts.reshape(far, ys * capacity, columns))
     acts = acts.reshape(xs, zs, ys, capacity, columns).transpose(0, 2, 1, 3, 4)
 
     grad_sent = for_plane(grad_own, grad_partner, experts, capacity)

time: 316 us -> 342 us (1.082)
  the two profiles are of different devices: /device:TPU:16 before, /device:TPU:8 now
where the time goes in v5:
time: 342 us; the launch traced here: 340 us
  starting transfers between devices  133 us (39%)
  waiting for transfers between devices  82.5 us (24%)
  blocking collectives  72.9 us (21%)
  between operations  14.8 us (4%)
  local copies, waits for them, and re-layouts  14.6 us (4%)
  Pallas kernels  11.4 us (3%)
  other arithmetic  5.58 us (2%)
  matrix products  4.87 us (1%)
    ppermute x8, starting transfers between devices, moved_acts(): got.append(lax.ppermute(piece, axes, pairs))  77.3 us
    all_to_all x2, blocking collectives, exchanged(): return lax.all_to_all(rows, axes, split_axis=0, concat_axis=0, tiled=True)  72.9 us
    all_to_all x4, waiting for transfers between devices, exchanged(): return lax.all_to_all(rows, axes, split_axis=0, concat_axis=0, tiled=True)  59.1 us
    all_to_all x4, starting transfers between devices, exchanged(): return lax.all_to_all(rows, axes, split_axis=0, concat_axis=0, tiled=True)  44.1 us
    ppermute x2, waiting for transfers between devices, shifted(): lax.ppermute(array, PIPE, [(i, (i + by) % sections) for i in range(sectio...  17.2 us
    pallas_call x2, Pallas kernels, experts_of(): pl.pallas_call(kernel, out_shape=pltpu.HBM((height_rows, width), jnp.bflo...  11.4 us
    unnamed x46, local copies, waits for them, and re-layouts  9.09 us
    ppermute x2, starting transfers between devices, swapped_rows(): return lax.ppermute(rows, 'zp', [(i, zs - 1 - i) for i in range(zs)])  7.91 us
  transfers between devices with their start and end apart: 17, of which 6 were waited for; matrix products, arithmetic and copies ran while one was open for 6% of the time, Pallas kernels for 3%

profile of v5, /device:TPU:8, one launch (start us, length us, event | category | flops | bytes accessed | tf_op | source)
XLA Modules:
  0.0 340.2 jit_solution(5946620654145743399)
XLA Ops:
  7.3 1.4 copy-done
  9.7 58.4 %all_to_all.30 = bf16[8,88,128]{2,1,0:T(8,128)(2,1)S(1)} all-to-all(bf16[8,88,128]{2,1,0:T(8,128)(2,1)S(1)} %pad_maximum_fusion), channel_id=1, replica_groups=mesh['x'=4,'zj'=4,'zp'=2,'y'=4,'zh'=4,'c'=2] {'zh','c'}, dimensions={0} | all-to-all | bytes 360448 | tf_op jit(solution)/shard_map/all_to_all | solution.py:64
  68.1 14.5 %all_to_all.31 = bf16[8,88,128]{2,1,0:T(8,128)(2,1)} all-to-all(bf16[8,88,128]{2,1,0:T(8,128)(2,1)S(1)} %all_to_all.30), channel_id=1, replica_groups=mesh['x'=4,'zj'=4,'zp'=2,'y'=4,'zh'=4,'c'=2] {'x','zp'}, dimensions={0} | all-to-all | bytes 360448 | tf_op jit(solution)/shard_map/all_to_all | solution.py:64
  83.5 1.4 collective-permute-start.3
  84.9 3.3 collective-permute-start.4
  88.2 16.2 %collective-permute-start.5 = (bf16[32,512]{1,0:T(8,128)(2,1)}, bf16[32,512]{1,0:T(8,128)(2,1)}, u32[]{:S(2)}, u32[]{:S(2)}) collective-permute-start(bf16[32,512]{1,0:T(8,128)(2,1)} %get-tuple-element.11), channel_id=1, source_target_pairs={{0,2},{1,34},{2,258},{3,290},{4,514},{5,546},{6,770},{7,802},{32,3... | collective-permute-start | bytes 98312 | tf_op jit(solution)/shard_map/ppermute | solution.py:236
  104.5 1.9 collective-permute-start.6
  107.1 2.5 collective-permute-start.2
  113.3 31.7 %collective-permute-start.7 = (bf16[32,512]{1,0:T(8,128)(2,1)}, bf16[32,512]{1,0:T(8,128)(2,1)}, u32[]{:S(2)}, u32[]{:S(2)}) collective-permute-start(bf16[32,512]{1,0:T(8,128)(2,1)} %get-tuple-element.9), channel_id=1, source_target_pairs={{0,4},{1,36},{2,260},{3,292},{4,516},{5,548},{6,772},{7,804},{32,5... | collective-permute-start | bytes 98312 | tf_op jit(solution)/shard_map/ppermute | solution.py:236
  145.8 1.9 collective-permute-start.8
  148.5 6.2 %collective-permute-done.2 = bf16[64,3584]{1,0:T(8,128)(2,1)} collective-permute-done((bf16[64,3584]{1,0:T(8,128)(2,1)S(1)}, bf16[64,3584]{1,0:T(8,128)(2,1)}, u32[]{:S(2)}, u32[]{:S(2)}) %collective-permute-start.2) | collective-permute-done | bytes 458784 | tf_op jit(solution)/shard_map/ppermute | solution.py:49
  154.7 5.4 %collective-permute-start = (bf16[64,3584]{1,0:T(8,128)(2,1)S(1)}, bf16[64,3584]{1,0:T(8,128)(2,1)}, u32[]{:S(2)}, u32[]{:S(2)}) collective-permute-start(bf16[64,3584]{1,0:T(8,128)(2,1)S(1)} %convolution_convert_fusion.1), channel_id=1, source_target_pairs={{0,32},{32,0},{1,33},{33,1},{2,34},{34,2},{3,35},{35,3},{4,36},{36... | collective-permute-start | bytes 1376264 | tf_op jit(solution)/shard_map/ppermute | solution.py:49
  160.2 1.1 broadcast_select_fusion.1
  161.4 1.5 broadcast_in_dim.10
  162.9 16.1 %all-to-all-start.4 = ((bf16[16,16,3584]{2,1,0:T(8,128)(2,1)}), bf16[16,16,3584]{2,1,0:T(8,128)(2,1)}, u32[]{:S(2)}, u32[]{:S(2)}) async-start(bf16[16,16,3584]{2,1,0:T(8,128)(2,1)} %bitcast.109), calls=%async_computation.4 | async-start | bytes 3670016 | tf_op jit(solution)/shard_map/all_to_all | solution.py:64
  179.1 14.9 %collective-permute-start.9 = (bf16[32,512]{1,0:T(8,128)(2,1)S(1)}, bf16[32,512]{1,0:T(8,128)(2,1)}, u32[]{:S(2)}, u32[]{:S(2)}) collective-permute-start(bf16[32,512]{1,0:T(8,128)(2,1)S(1)} %get-tuple-element.7), channel_id=1, source_target_pairs={{0,6},{1,38},{2,262},{3,294},{4,518},{5,550},{6,774},{7,806},{32,7... | collective-permute-start | bytes 98312 | tf_op jit(solution)/shard_map/ppermute | solution.py:236
  194.7 5.8 %collective-permute-start.10 = (bf16[32,512]{1,0:T(8,128)(2,1)S(1)}, bf16[32,512]{1,0:T(8,128)(2,1)}, u32[]{:S(2)}, u32[]{:S(2)}) collective-permute-start(bf16[32,512]{1,0:T(8,128)(2,1)S(1)} %get-tuple-element.6), channel_id=1, source_target_pairs={{0,7},{1,39},{2,263},{3,295},{4,519},{5,551},{6,775},{7,807},{32,6... | collective-permute-start | bytes 98312 | tf_op jit(solution)/shard_map/ppermute | solution.py:236
  202.6 1.8 all-to-all-done.4
  204.4 1.5 broadcast_in_dim.8
  205.8 15.0 %all-to-all-start = ((bf16[16,16,3584]{2,1,0:T(8,128)(2,1)}), bf16[16,16,3584]{2,1,0:T(8,128)(2,1)}, u32[]{:S(2)}, u32[]{:S(2)}) async-start(bf16[16,16,3584]{2,1,0:T(8,128)(2,1)} %bitcast.108), calls=%async_computation | async-start | bytes 3670016 | tf_op jit(solution)/shard_map/all_to_all | solution.py:64
  224.1 5.8 %shard_map.141 = bf16[256,3584]{1,0:T(8,128)(2,1)} custom-call(bf16[256,3584]{1,0:T(8,128)(2,1)} %bitcast.27.rows_hbm, bf16[32,8,88,128]{3,2,1,0:T(8,128)(2,1)} %bitcast.104, bf16[256,512]{1,0:T(8,128)(2,1)S(1)} %bitcast.103), custom_call_target="tpu_custom_call" | custom-call | flops 1409286144 | bytes 5767168 | tf_op jit(solution)/shard_map/pallas_call | solution.py:196
  229.9 12.3 %all-to-all-done = bf16[16,16,3584]{2,1,0:T(8,128)(2,1)} async-done(((bf16[16,16,3584]{2,1,0:T(8,128)(2,1)}), bf16[16,16,3584]{2,1,0:T(8,128)(2,1)}, u32[]{:S(2)}, u32[]{:S(2)}) %all-to-all-start) | async-done | bytes 1835040 | tf_op jit(solution)/shard_map/all_to_all | solution.py:64
  242.2 6.6 %all-to-all-start.5 = ((bf16[32,8,3584]{2,1,0:T(8,128)(2,1)}), bf16[32,8,3584]{2,1,0:T(8,128)(2,1)}, u32[]{:S(2)}, u32[]{:S(2)}) async-start(bf16[32,8,3584]{2,1,0:T(8,128)(2,1)} %bitcast.107), calls=%async_computation.5 | async-start | bytes 3670016 | tf_op jit(solution)/shard_map/all_to_all | solution.py:64
  248.8 5.6 %shard_map.140 = bf16[256,3584]{1,0:T(8,128)(2,1)} custom-call(bf16[256,3584]{1,0:T(8,128)(2,1)} %bitcast.8.rows_hbm, bf16[32,8,88,128]{3,2,1,0:T(8,128)(2,1)} %bitcast.105), custom_call_target="tpu_custom_call" | custom-call | flops 1409286144 | bytes 5767168 | tf_op jit(solution)/shard_map/pallas_call | solution.py:196
  254.4 21.2 %all-to-all-done.5 = bf16[32,8,3584]{2,1,0:T(8,128)(2,1)} async-done(((bf16[32,8,3584]{2,1,0:T(8,128)(2,1)}), bf16[32,8,3584]{2,1,0:T(8,128)(2,1)}, u32[]{:S(2)}, u32[]{:S(2)}) %all-to-all-start.5) | async-done | bytes 1835040 | tf_op jit(solution)/shard_map/all_to_all | solution.py:64
  275.6 6.4 %all-to-all-start.3 = ((bf16[32,8,3584]{2,1,0:T(8,128)(2,1)}), bf16[32,8,3584]{2,1,0:T(8,128)(2,1)}, u32[]{:S(2)}, u32[]{:S(2)}) async-start(bf16[32,8,3584]{2,1,0:T(8,128)(2,1)} %bitcast.106), calls=%async_computation.3 | async-start | bytes 3670016 | tf_op jit(solution)/shard_map/all_to_all | solution.py:64
  282.2 2.1 fusion.8
  284.7 2.1 collective-permute-start.11
  286.8 23.9 %all-to-all-done.3 = bf16[32,8,3584]{2,1,0:T(8,128)(2,1)} async-done(((bf16[32,8,3584]{2,1,0:T(8,128)(2,1)}), bf16[32,8,3584]{2,1,0:T(8,128)(2,1)}, u32[]{:S(2)}, u32[]{:S(2)}) %all-to-all-start.3) | async-done | bytes 1835040 | tf_op jit(solution)/shard_map/all_to_all | solution.py:64
  310.7 2.0 fusion.3
  312.7 1.9 collective-permute-start.1
  314.6 17.1 %collective-permute-done.1 = bf16[1,64,3584]{2,1,0:T(8,128)(2,1)S(1)} collective-permute-done((bf16[1,64,3584]{2,1,0:T(8,128)(2,1)S(1)}, bf16[1,64,3584]{2,1,0:T(8,128)(2,1)S(1)}, u32[]{:S(2)}, u32[]{:S(2)}) %collective-permute-start.1) | collective-permute-done | bytes 458784 | tf_op jit(solution)/shard_map/ppermute | solution.py:251
  (84 shorter events, 15.7 us)
Async XLA Ops:
  7.2 1.5 copy-start
  7.2 75.6 %copy-start.5 = (bf16[1,1,256,512]{3,2,1,0:T(8,128)(2,1)S(1)}, bf16[1,1,256,512]{3,2,1,0:T(8,128)(2,1)}, u32[]{:S(2)}) copy-start(bf16[1,1,256,512]{3,2,1,0:T(8,128)(2,1)} %param.20) | copy-start | bytes 786436
  7.2 99.2 %copy-start.14 = (s32[1,64,1]{1,2,0:T(1,128)S(1)}, s32[1,64,1]{1,2,0:T(1,128)}, u32[]{:S(2)}) copy-start(s32[1,64,1]{1,2,0:T(1,128)} %param.17) | copy-start | bytes 772
  7.2 99.4 %copy-start.3 = (bf16[1,64,3584]{2,1,0:T(8,128)(2,1)S(1)}, bf16[1,64,3584]{2,1,0:T(8,128)(2,1)}, u32[]{:S(2)}) copy-start(bf16[1,64,3584]{2,1,0:T(8,128)(2,1)} %param.16) | copy-start | bytes 1376260
  7.2 216.9 %all-gather.3.cloned.1.call-start = ((), (), s32[]{:S(2)}) async-start(), calls=%async_computation.6 | async-start | bytes 5947392 | tf_op jit(solution)/shard_map/all_gather | solution.py:283
  8.7 102.6 %copy-start.1 = (bf16[1,64,3584]{2,1,0:T(8,128)(2,1)S(1)}, bf16[1,64,3584]{2,1,0:T(8,128)(2,1)}, u32[]{:S(2)}) copy-start(bf16[1,64,3584]{2,1,0:T(8,128)(2,1)} %param.13) | copy-start | bytes 1376260
  83.5 29.2 %collective-permute-start.3 = (bf16[32,512]{1,0:T(8,128)(2,1)}, bf16[32,512]{1,0:T(8,128)(2,1)S(1)}, u32[]{:S(2)}, u32[]{:S(2)}) collective-permute-start(bf16[32,512]{1,0:T(8,128)(2,1)} %get-tuple-element.13), channel_id=1, source_target_pairs={{0,0},{1,32},{2,256},{3,288},{4,512},{5,544},{6,768},{7,800},{32,1... | collective-permute-start | bytes 98312 | tf_op jit(solution)/shard_map/ppermute | solution.py:236
  84.9 60.9 %collective-permute-start.4 = (bf16[32,512]{1,0:T(8,128)(2,1)}, bf16[32,512]{1,0:T(8,128)(2,1)}, u32[]{:S(2)}, u32[]{:S(2)}) collective-permute-start(bf16[32,512]{1,0:T(8,128)(2,1)} %get-tuple-element.12), channel_id=1, source_target_pairs={{0,1},{1,33},{2,257},{3,289},{4,513},{5,545},{6,769},{7,801},{32,0... | collective-permute-start | bytes 98312 | tf_op jit(solution)/shard_map/ppermute | solution.py:236
  88.2 90.8 %collective-permute-start.5 = (bf16[32,512]{1,0:T(8,128)(2,1)}, bf16[32,512]{1,0:T(8,128)(2,1)}, u32[]{:S(2)}, u32[]{:S(2)}) collective-permute-start(bf16[32,512]{1,0:T(8,128)(2,1)} %get-tuple-element.11), channel_id=1, source_target_pairs={{0,2},{1,34},{2,258},{3,290},{4,514},{5,546},{6,770},{7,802},{32,3... | collective-permute-start | bytes 98312 | tf_op jit(solution)/shard_map/ppermute | solution.py:236
  104.5 90.2 %collective-permute-start.6 = (bf16[32,512]{1,0:T(8,128)(2,1)}, bf16[32,512]{1,0:T(8,128)(2,1)}, u32[]{:S(2)}, u32[]{:S(2)}) collective-permute-start(bf16[32,512]{1,0:T(8,128)(2,1)} %get-tuple-element.10), channel_id=1, source_target_pairs={{0,3},{1,35},{2,259},{3,291},{4,515},{5,547},{6,771},{7,803},{32,2... | collective-permute-start | bytes 98312 | tf_op jit(solution)/shard_map/ppermute | solution.py:236
  106.6 0.5 copy-start.10
  107.1 47.6 %collective-permute-start.2 = (bf16[64,3584]{1,0:T(8,128)(2,1)S(1)}, bf16[64,3584]{1,0:T(8,128)(2,1)}, u32[]{:S(2)}, u32[]{:S(2)}) collective-permute-start(bf16[64,3584]{1,0:T(8,128)(2,1)S(1)} %convolution_convert_fusion), channel_id=1, source_target_pairs={{0,32},{32,0},{1,33},{33,1},{2,34},{34,2},{3,35},{35,3},{4,36},{36... | collective-permute-start | bytes 1376264 | tf_op jit(solution)/shard_map/ppermute | solution.py:49
  112.2 0.6 copy-start.8
  112.7 0.6 copy-start.6
  113.3 107.5 %collective-permute-start.7 = (bf16[32,512]{1,0:T(8,128)(2,1)}, bf16[32,512]{1,0:T(8,128)(2,1)}, u32[]{:S(2)}, u32[]{:S(2)}) collective-permute-start(bf16[32,512]{1,0:T(8,128)(2,1)} %get-tuple-element.9), channel_id=1, source_target_pairs={{0,4},{1,36},{2,260},{3,292},{4,516},{5,548},{6,772},{7,804},{32,5... | collective-permute-start | bytes 98312 | tf_op jit(solution)/shard_map/ppermute | solution.py:236
  145.8 75.8 %collective-permute-start.8 = (bf16[32,512]{1,0:T(8,128)(2,1)}, bf16[32,512]{1,0:T(8,128)(2,1)}, u32[]{:S(2)}, u32[]{:S(2)}) collective-permute-start(bf16[32,512]{1,0:T(8,128)(2,1)} %get-tuple-element.8), channel_id=1, source_target_pairs={{0,5},{1,37},{2,261},{3,293},{4,517},{5,549},{6,773},{7,805},{32,4... | collective-permute-start | bytes 98312 | tf_op jit(solution)/shard_map/ppermute | solution.py:236
  154.7 46.6 %collective-permute-start = (bf16[64,3584]{1,0:T(8,128)(2,1)S(1)}, bf16[64,3584]{1,0:T(8,128)(2,1)}, u32[]{:S(2)}, u32[]{:S(2)}) collective-permute-start(bf16[64,3584]{1,0:T(8,128)(2,1)S(1)} %convolution_convert_fusion.1), channel_id=1, source_target_pairs={{0,32},{32,0},{1,33},{33,1},{2,34},{34,2},{3,35},{35,3},{4,36},{36... | collective-permute-start | bytes 1376264 | tf_op jit(solution)/shard_map/ppermute | solution.py:49
  162.9 41.5 %all-to-all-start.4 = ((bf16[16,16,3584]{2,1,0:T(8,128)(2,1)}), bf16[16,16,3584]{2,1,0:T(8,128)(2,1)}, u32[]{:S(2)}, u32[]{:S(2)}) async-start(bf16[16,16,3584]{2,1,0:T(8,128)(2,1)} %bitcast.109), calls=%async_computation.4 | async-start | bytes 3670016 | tf_op jit(solution)/shard_map/all_to_all | solution.py:64
  179.1 43.3 %collective-permute-start.9 = (bf16[32,512]{1,0:T(8,128)(2,1)S(1)}, bf16[32,512]{1,0:T(8,128)(2,1)}, u32[]{:S(2)}, u32[]{:S(2)}) collective-permute-start(bf16[32,512]{1,0:T(8,128)(2,1)S(1)} %get-tuple-element.7), channel_id=1, source_target_pairs={{0,6},{1,38},{2,262},{3,294},{4,518},{5,550},{6,774},{7,806},{32,7... | collective-permute-start | bytes 98312 | tf_op jit(solution)/shard_map/ppermute | solution.py:236
  194.7 28.4 %collective-permute-start.10 = (bf16[32,512]{1,0:T(8,128)(2,1)S(1)}, bf16[32,512]{1,0:T(8,128)(2,1)}, u32[]{:S(2)}, u32[]{:S(2)}) collective-permute-start(bf16[32,512]{1,0:T(8,128)(2,1)S(1)} %get-tuple-element.6), channel_id=1, source_target_pairs={{0,7},{1,39},{2,263},{3,295},{4,519},{5,551},{6,775},{7,807},{32,6... | collective-permute-start | bytes 98312 | tf_op jit(solution)/shard_map/ppermute | solution.py:236
  205.8 36.4 %all-to-all-start = ((bf16[16,16,3584]{2,1,0:T(8,128)(2,1)}), bf16[16,16,3584]{2,1,0:T(8,128)(2,1)}, u32[]{:S(2)}, u32[]{:S(2)}) async-start(bf16[16,16,3584]{2,1,0:T(8,128)(2,1)} %bitcast.108), calls=%async_computation | async-start | bytes 3670016 | tf_op jit(solution)/shard_map/all_to_all | solution.py:64
  242.2 33.4 %all-to-all-start.5 = ((bf16[32,8,3584]{2,1,0:T(8,128)(2,1)}), bf16[32,8,3584]{2,1,0:T(8,128)(2,1)}, u32[]{:S(2)}, u32[]{:S(2)}) async-start(bf16[32,8,3584]{2,1,0:T(8,128)(2,1)} %bitcast.107), calls=%async_computation.5 | async-start | bytes 3670016 | tf_op jit(solution)/shard_map/all_to_all | solution.py:64
  275.6 6.4 %copy-start.2 = (bf16[1,64,3584]{2,1,0:T(8,128)(2,1)S(1)}, bf16[1,64,3584]{2,1,0:T(8,128)(2,1)}, u32[]{:S(2)}) copy-start(bf16[1,64,3584]{2,1,0:T(8,128)(2,1)} %param.19) | copy-start | bytes 1376260
  275.6 6.7 %copy-start.7 = (s32[256]{0:T(256)S(1)}, s32[256]{0:T(256)}, u32[]{:S(2)}) copy-start(s32[256]{0:T(256)} %constant.200) | copy-start | bytes 3076
  275.6 6.7 %copy-start.11 = (s32[64]{0:T(128)S(1)}, s32[64]{0:T(128)}, u32[]{:S(2)}) copy-start(s32[64]{0:T(128)} %copy-done.10) | copy-start | bytes 772
  275.6 6.7 %copy-start.13 = (f32[1,64,1]{1,2,0:T(1,128)S(1)}, f32[1,64,1]{1,2,0:T(1,128)}, u32[]{:S(2)}) copy-start(f32[1,64,1]{1,2,0:T(1,128)} %param.18) | copy-start | bytes 772
  275.6 35.1 %all-to-all-start.3 = ((bf16[32,8,3584]{2,1,0:T(8,128)(2,1)}), bf16[32,8,3584]{2,1,0:T(8,128)(2,1)}, u32[]{:S(2)}, u32[]{:S(2)}) async-start(bf16[32,8,3584]{2,1,0:T(8,128)(2,1)} %bitcast.106), calls=%async_computation.3 | async-start | bytes 3670016 | tf_op jit(solution)/shard_map/all_to_all | solution.py:64
  282.0 2.4 copy-start.4
  284.3 26.4 %copy-start.9 = (s32[64]{0:T(128)S(1)}, s32[64]{0:T(128)}, u32[]{:S(2)}) copy-start(s32[64]{0:T(128)} %copy-done.8) | copy-start | bytes 772
  284.4 26.4 %copy-start.12 = (f32[1,64,1]{1,2,0:T(1,128)S(1)}, f32[1,64,1]{1,2,0:T(1,128)}, u32[]{:S(2)}) copy-start(f32[1,64,1]{1,2,0:T(1,128)} %param.15) | copy-start | bytes 772
  284.7 29.9 %collective-permute-start.11 = (bf16[1,64,3584]{2,1,0:T(8,128)(2,1)S(1)}, bf16[1,64,3584]{2,1,0:T(8,128)(2,1)S(1)}, u32[]{:S(2)}, u32[]{:S(2)}) collective-permute-start(bf16[1,64,3584]{2,1,0:T(8,128)(2,1)S(1)} %fusion.18), channel_id=1, source_target_pairs={{0,992},{32,0},{64,32},{96,64},{128,96},{160,128},{192,160},{224,1... | collective-permute-start | bytes 1376264 | tf_op jit(solution)/shard_map/ppermute | solution.py:251
  312.7 19.1 %collective-permute-start.1 = (bf16[1,64,3584]{2,1,0:T(8,128)(2,1)S(1)}, bf16[1,64,3584]{2,1,0:T(8,128)(2,1)S(1)}, u32[]{:S(2)}, u32[]{:S(2)}) collective-permute-start(bf16[1,64,3584]{2,1,0:T(8,128)(2,1)S(1)} %fusion.3), channel_id=1, source_target_pairs={{0,32},{32,64},{64,96},{96,128},{128,160},{160,192},{192,224},{224... | collective-permute-start | bytes 1376264 | tf_op jit(solution)/shard_map/ppermute | solution.py:251
Sparse Core Ops, SparseCore 0:
  82.8 129.5 all-gather.2
